TPU v7x, 32 devices: a 4x4x1 block of a 4x4x8 slice. The times are simulated.
32 devices in a mesh: data: 1 (over z), cp: 4 (over y), tp: 8 (over x, core).
Axes of the slice: x: 4, y: 4, z: 1, core: 2. Of those that a mesh axis runs over, the one named last changes fastest.
The devices are a block of a 4x4x8 slice.
Arguments:
- act_in: bfloat16 [2, 4096, 2048], P(None, ('data', 'cp', 'tp'))
- route_ids: int32 [2, 4096, 2], P(None, ('data', 'cp', 'tp'))
- route_gates: float32 [2, 4096, 2], P(None, ('data', 'cp', 'tp'))
- w_query: bfloat16 [2048, 16, 128], P(None, 'tp')
- w_key: bfloat16 [2048, 16, 128], P(None, 'tp')
- w_value: bfloat16 [2048, 16, 128], P(None, 'tp')
- w_out: bfloat16 [16, 128, 2048], P('tp')
- w_gate: bfloat16 [32, 2048, 1408], P(('cp', 'tp'))
- w_up: bfloat16 [32, 2048, 1408], P(('cp', 'tp'))
- w_down: bfloat16 [32, 1408, 2048], P(('cp', 'tp'))
Outputs:
- output: bfloat16 [2, 4096, 2048], P(None, ('data', 'cp', 'tp'))
All inputs are finite; a program needn't handle non-finite values.
Results may differ from a plain program's by a relative error of at most 0.00522276.
Values are sent between devices in bfloat16 or wider.
A program may use at most 768 MiB of HBM per device.

v0:
```python
import jax
import jax.numpy as jnp
from jax import lax
from jax.sharding import PartitionSpec as P


def pick_rows(row_table, row_ids):
    return jnp.take(row_table, row_ids, axis=0, mode='fill', fill_value=0)


def attend_local(act_in, w_query, w_key, w_value, w_out, cp_size, tp_size):
    n_micro, tokens, hidden = act_in.shape
    q_local, head_dim = w_query.shape[1], w_query.shape[2]
    kv_local = w_key.shape[1]
    group_size = q_local // kv_local
    half_rows = tokens * tp_size
    piece_len = half_rows // 2
    seq_len = half_rows * cp_size
    cp_rank = lax.axis_index('cp')
    x_half = lax.all_gather(act_in, 'tp', axis=1, tiled=True)
    query_rows = jnp.einsum('bsh,hnd->bsnd', x_half, w_query, preferred_element_type=jnp.float32).astype(jnp.bfloat16)
    query_rows = query_rows.reshape(n_micro, half_rows, kv_local, group_size, head_dim)
    key_half = jnp.einsum('bsh,hnd->bsnd', x_half, w_key, preferred_element_type=jnp.float32).astype(jnp.bfloat16)
    value_half = jnp.einsum('bsh,hnd->bsnd', x_half, w_value, preferred_element_type=jnp.float32).astype(jnp.bfloat16)
    key_all = lax.all_gather(key_half, 'cp', axis=1, tiled=True)
    value_all = lax.all_gather(value_half, 'cp', axis=1, tiled=True)
    local_ix = jnp.arange(half_rows)
    owner_ix = jnp.arange(cp_size)[:, None]
    key_pos = jnp.where(local_ix < piece_len, owner_ix * piece_len + local_ix, (2 * cp_size - 1 - owner_ix) * piece_len + local_ix - piece_len).reshape(seq_len)
    score_scale = head_dim ** -0.5
    halves = []
    for half_id in range(2):
        piece_id = cp_rank if half_id == 0 else 2 * cp_size - 1 - cp_rank
        query_pos = piece_id * piece_len + jnp.arange(piece_len)
        q_part = query_rows[:, half_id * piece_len:(half_id + 1) * piece_len]
        scores = jnp.einsum('bqhgd,bkhd->bhgqk', q_part, key_all, preferred_element_type=jnp.float32) * score_scale
        scores = jnp.where(key_pos[None, :] <= query_pos[:, None], scores, -jnp.inf)
        row_peak = jnp.max(scores, axis=-1, keepdims=True)
        exp_scores = jnp.exp(scores - row_peak)
        row_sum = jnp.sum(exp_scores, axis=-1)
        weighted = jnp.einsum('bhgqk,bkhd->bqhgd', exp_scores.astype(jnp.bfloat16), value_all, preferred_element_type=jnp.float32)
        weighted = weighted / jnp.transpose(row_sum, (0, 3, 1, 2))[..., None]
        halves.append(weighted.astype(jnp.bfloat16))
    attn_rows = jnp.concatenate(halves, axis=1).reshape(n_micro, half_rows, q_local, head_dim)
    partial = jnp.einsum('bsnd,ndh->bsh', attn_rows, w_out, preferred_element_type=jnp.float32)
    attn_sum = lax.psum_scatter(partial, 'tp', scatter_dimension=1, tiled=True)
    return (act_in.astype(jnp.float32) + attn_sum).astype(jnp.bfloat16)


def dispatch_experts(mid_rows, route_ids, route_gates, w_gate, w_up, w_down, experts):
    n_micro, tokens, hidden = mid_rows.shape
    capacity = (4 * tokens) // experts
    flat_ids = route_ids.reshape(n_micro, 2 * tokens)
    expert_hits = (flat_ids[..., None] == jnp.arange(experts)).astype(jnp.int32)
    slot_rank = jnp.sum((jnp.cumsum(expert_hits, axis=1) - 1) * expert_hits, axis=-1)
    dest_slot = flat_ids * capacity + slot_rank
    micro_ix = jnp.arange(n_micro)[:, None]
    token_of = jnp.broadcast_to((jnp.arange(2 * tokens, dtype=jnp.int32) // 2)[None, :], dest_slot.shape)
    source_row = jnp.full((n_micro, experts * capacity), tokens, jnp.int32).at[micro_ix, dest_slot].set(token_of)
    send_buf = jax.vmap(pick_rows)(mid_rows, source_row).reshape(n_micro, experts, capacity, hidden)
    recv_buf = lax.all_to_all(send_buf, ('cp', 'tp'), 1, 1, tiled=True)
    expert_in = recv_buf.reshape(n_micro, experts * capacity, hidden)
    gate_act = jnp.einsum('bth,hf->btf', expert_in, w_gate[0], preferred_element_type=jnp.float32)
    up_act = jnp.einsum('bth,hf->btf', expert_in, w_up[0], preferred_element_type=jnp.float32)
    mixed_act = (jax.nn.silu(gate_act) * up_act).astype(jnp.bfloat16)
    expert_out = jnp.einsum('btf,fh->bth', mixed_act, w_down[0], preferred_element_type=jnp.float32).astype(jnp.bfloat16)
    back_buf = lax.all_to_all(expert_out.reshape(n_micro, experts, capacity, hidden), ('cp', 'tp'), 1, 1, tiled=True)
    picked = jax.vmap(pick_rows)(back_buf.reshape(n_micro, experts * capacity, hidden), dest_slot).reshape(n_micro, tokens, 2, hidden)
    combined = route_gates[:, :, 0:1] * picked[:, :, 0].astype(jnp.float32) + route_gates[:, :, 1:2] * picked[:, :, 1].astype(jnp.float32)
    return (mid_rows.astype(jnp.float32) + combined).astype(jnp.bfloat16)


def solution(mesh):
    cp_size = mesh.shape['cp']
    tp_size = mesh.shape['tp']
    experts = cp_size * tp_size
    row_spec = P(None, ('data', 'cp', 'tp'), None)
    head_spec = P(None, 'tp', None)
    out_spec = P('tp', None, None)
    expert_spec = P(('cp', 'tp'), None, None)

    def device_step(act_in, route_ids, route_gates, w_query, w_key, w_value, w_out, w_gate, w_up, w_down):
        mid_rows = attend_local(act_in, w_query, w_key, w_value, w_out, cp_size, tp_size)
        return dispatch_experts(mid_rows, route_ids, route_gates, w_gate, w_up, w_down, experts)

    return jax.shard_map(device_step, mesh=mesh, in_specs=(row_spec, row_spec, row_spec, head_spec, head_spec, head_spec, out_spec, expert_spec, expert_spec, expert_spec), out_specs=row_spec, check_vma=False)
```

profile of v0, /device:TPU:97, one launch (start us, length us, event | category | flops | bytes accessed | tf_op | source)
XLA Modules:
  0.0 519.7 jit_solution(11467006741323226763)
XLA Ops:
  6.6 0.7 all-gather.4.cloned.1.call-update
  7.4 52.9 %all-gather.4.cloned.1.call-done = bf16[2,1024,2048]{2,1,0:T(8,128)(2,1)} async-done(((bf16[2,128,2048]{2,1,0:T(8,128)(2,1)}), bf16[2,1024,2048]{2,1,0:T(8,128)(2,1)}) %all-gather.4.cloned.1.call-update) | async-done | bytes 8388624 | tf_op jit(solution)/shard_map/all_gather | solution.py:20
  60.2 7.0 %fusion.37 = bf16[2,1024,2,128]{3,1,2,0:T(8,128)(2,1)} fusion(bf16[2,1024,2048]{2,1,0:T(8,128)(2,1)} %all-gather.4.cloned.1.call-done, bf16[2048,2,128]{2,1,0:T(2,128)(2,1)} %param.14), kind=kOutput, calls=%fused_computation.45 | convolution fusion | flops 2148007936 | bytes 10485760 | tf_op jit(solution)/shard_map/bsh,hnd->bsnd/dot_general | solution.py:23
  67.3 0.1 all-gather.6.cloned.1.call-start
  67.4 0.1 fusion.81
  67.5 3.6 broadcast_compare_fusion.1
  71.1 6.9 %fusion.34 = bf16[2,1024,2,128]{3,1,2,0:T(8,128)(2,1)} fusion(bf16[2,1024,2048]{2,1,0:T(8,128)(2,1)} %all-gather.4.cloned.1.call-done, bf16[2048,2,128]{2,1,0:T(2,128)(2,1)} %param.15), kind=kOutput, calls=%fused_computation.44 | convolution fusion | flops 2148007936 | bytes 10485760 | tf_op jit(solution)/shard_map/bsh,hnd->bsnd/dot_general | solution.py:24
  78.1 0.5 reduce-scatter.2.cloned.1.call-start
  78.6 6.9 %fusion.43 = bf16[2,1024,2,1,128]{4,1,2,0,3:T(8,128)(2,1)} fusion(bf16[2,1024,2048]{2,1,0:T(8,128)(2,1)} %all-gather.4.cloned.1.call-done, bf16[2048,2,128]{2,1,0:T(2,128)(2,1)} %param.13), kind=kOutput, calls=%fused_computation.47 | convolution fusion | flops 2148007936 | bytes 10485760 | tf_op jit(solution)/shard_map/bsh,hnd->bsnd/dot_general | solution.py:21
  85.6 27.0 %all-gather.8.cloned.1.call-done = bf16[2,4096,2,128]{3,1,2,0:T(8,128)(2,1)} async-done(((bf16[2,1024,2,128]{3,1,2,0:T(8,128)(2,1)}), bf16[2,4096,2,128]{3,1,2,0:T(8,128)(2,1)}) %all-gather.8.cloned.1.call-update) | async-done | bytes 4194320 | tf_op jit(solution)/shard_map/all_gather | solution.py:25
  112.6 15.7 %fusion.5 = (f32[2,2,512]{2,1,0:T(2,128)S(1)}, f32[2,2,4096,512]{3,2,1,0:T(8,128)}) fusion(pred[512,4096]{0,1:T(8,128)(4,1)} %get-tuple-element.6, bf16[2,4096,2,128]{3,1,2,0:T(8,128)(2,1)} %all-gather.8.cloned.1.call-done, bf16[2,1024,2,1,128]{4,1,2,0,3:T(8,128)(2,1)} %fusion.43), kind=kOutput, calls=%fused_computation.12 | convolution fusion | flops 2172647424 | bytes 40378368 | tf_op jit(solution)/shard_map/bqhgd,bkhd->bhgqk/dot_general | solution.py:36
  128.3 15.9 %fusion.4 = (f32[2,2,512]{2,1,0:T(2,128)S(1)}, f32[2,2,4096,512]{3,2,1,0:T(8,128)}) fusion(pred[512,4096]{0,1:T(8,128)(4,1)S(1)} %get-tuple-element.5, bf16[2,4096,2,128]{3,1,2,0:T(8,128)(2,1)} %all-gather.8.cloned.1.call-done, bf16[2,1024,2,1,128]{4,1,2,0,3:T(8,128)(2,1)S(1)} %copy-done.8), kind=kOutput, calls=%fused_computation.11 | convolution fusion | flops 2172647424 | bytes 40378368 | tf_op jit(solution)/shard_map/bqhgd,bkhd->bhgqk/dot_general | solution.py:36
  144.1 15.1 %fusion.2 = f32[2,2,512]{2,1,0:T(2,128)S(1)} fusion(f32[2,2,4096,512]{3,2,1,0:T(8,128)} %get-tuple-element.12, f32[2,2,512]{2,1,0:T(2,128)S(1)} %get-tuple-element.11, pred[512,4096]{0,1:T(8,128)(4,1)S(1)} %copy-done.3), kind=kLoop, calls=%fused_computation.9 | loop fusion | flops 33552384 | bytes 35667968 | tf_op jit(solution)/shard_map/reduce_sum | solution.py:40
  159.3 5.2 copy-done.2
  164.4 7.3 %fusion = f32[2,2,512]{2,1,0:T(2,128)S(1)} fusion(f32[2,2,4096,512]{3,2,1,0:T(8,128)S(1)} %copy-done.2, f32[2,2,512]{2,1,0:T(2,128)S(1)} %get-tuple-element.13, pred[512,4096]{0,1:T(8,128)(4,1)S(1)} %get-tuple-element.5), kind=kLoop, calls=%fused_computation.7 | loop fusion | flops 33552384 | bytes 35667968 | tf_op jit(solution)/shard_map/reduce_sum | solution.py:40
  171.7 17.9 %fusion.61 = bf16[2,512,2,1,128]{1,4,2,0,3:T(8,128)(2,1)} fusion(bf16[2,4096,2,128]{3,1,2,0:T(8,128)(2,1)} %all-gather.6.cloned.1.call-done, f32[2,2,4096,512]{3,2,1,0:T(8,128)} %get-tuple-element.12, f32[2,2,512]{2,1,0:T(2,128)S(1)} %get-tuple-element.11, pred[512,4096]{0,1:T(8,128)(4,1)} %get-tuple-element.6, f32[2,512,2]{1,2,0:T(2,128)S(1)} %bitcast.227), kind=kOutput, calls=%fused_computation.53 | convolution fusion | flops 2181562368 | bytes 40386560 | tf_op jit(solution)/shard_map/bhgqk,bkhd->bqhgd/dot_general | solution.py:41
  189.6 17.5 %fusion.55 = bf16[2,512,2,1,128]{1,4,2,0,3:T(8,128)(2,1)} fusion(bf16[2,4096,2,128]{3,1,2,0:T(8,128)(2,1)} %all-gather.6.cloned.1.call-done, f32[2,2,4096,512]{3,2,1,0:T(8,128)} %get-tuple-element.14, f32[2,2,512]{2,1,0:T(2,128)S(1)} %get-tuple-element.13, pred[512,4096]{0,1:T(8,128)(4,1)S(1)} %get-tuple-element.5, f32[2,512,2]{1,2,0:T(2,128)S(1)} %bitcast.226), kind=kOutput, calls=%fused_computation.51 | convolution fusion | flops 2181562368 | bytes 40386560 | tf_op jit(solution)/shard_map/bhgqk,bkhd->bqhgd/dot_general | solution.py:41
  207.1 9.3 %convolution_bitcast_fusion = f32[2,1024,2048]{2,1,0:T(8,128)} fusion(bf16[2,512,2,1,128]{1,4,2,0,3:T(8,128)(2,1)} %fusion.61, bf16[2,512,2,1,128]{1,4,2,0,3:T(8,128)(2,1)} %fusion.55, bf16[2,128,2048]{2,1,0:T(8,128)(2,1)S(1)} %copy-done), kind=kOutput, calls=%fused_computation.25 | convolution fusion | flops 2149580800 | bytes 18874368 | tf_op jit(solution)/shard_map/bsnd,ndh->bsh/dot_general | solution.py:45
  216.5 0.6 copy-done.6
  217.1 0.1 copy.61
  217.2 0.1 reshape.202
  217.4 0.1 eq.26
  217.5 0.1 copy.66
  217.7 0.1 mul.108
  217.8 1.2 reduce-window.6
  219.0 0.2 slice_reduce_fusion
  219.3 0.1 fusion.78
  219.5 24.5 %scatter_fusion = s32[2,512]{1,0:T(2,128)S(1)} fusion(s32[2,512]{1,0:T(2,128)S(1)} %broadcast_in_dim.73, s32[512]{0:T(512)S(1)} %bitcast.219, s32[512]{0:T(512)S(1)} %bitcast.225), kind=kCustom, calls=%fused_computation.2 | custom fusion | bytes 10240 | tf_op jit(solution)/shard_map/scatter | solution.py:59
  244.0 0.1 broadcast_in_dim.76
  244.1 61.9 %reduce-scatter.2.cloned.1.call-done = f32[2,128,2048]{2,1,0:T(8,128)} async-done(((f32[2,1024,2048]{2,1,0:T(8,128)}), f32[2,128,2048]{2,1,0:T(8,128)}) %reduce-scatter.2.cloned.1.call-update) | async-done | bytes 2097168 | tf_op jit(solution)/shard_map/reduce_scatter | solution.py:46
  306.0 1.9 add_convert_fusion
  307.9 22.3 %gather_fusion = bf16[1024,2048]{1,0:T(8,128)(2,1)} fusion(bf16[2,128,2048]{2,1,0:T(8,128)(2,1)S(1)} %add_convert_fusion, s32[1024]{0:T(1024)S(1)} %bitcast.217), kind=kCustom, calls=%fused_computation | custom fusion | bytes 8396800 | tf_op jit(solution)/shard_map/vmap(jit(_take))/gather | solution.py:8
  330.2 2.5 copy_select_fusion
  332.7 61.0 %all_to_all.10 = bf16[2,32,16,2048]{3,2,0,1:T(8,128)(2,1)S(1)} all-to-all(bf16[2,32,16,2048]{3,2,0,1:T(8,128)(2,1)S(1)} %copy_select_fusion), channel_id=1, replica_groups=mesh['data'=1,'cp'=4,'tp'=8] {'cp','tp'}, dimensions={1} | all-to-all | bytes 8388608 | tf_op jit(solution)/shard_map/all_to_all | solution.py:61
  393.7 0.6 copy.69
  394.3 2.1 copy-done.4
  396.4 8.4 %fusion.22 = f32[2,512,1408]{2,1,0:T(8,128)} fusion(bf16[2,512,2048]{2,1,0:T(8,128)(2,1)S(1)} %bitcast.221, bf16[1,2048,1408]{2,1,0:T(8,128)(2,1)S(1)} %bitcast.231), kind=kOutput, calls=%fused_computation.28 | convolution fusion | flops 5905580032 | bytes 15728640 | tf_op jit(solution)/shard_map/bth,hf->btf/dot_general | solution.py:64
  404.8 20.9 %fusion.28 = bf16[2,512,2048]{2,1,0:T(8,128)(2,1)} fusion(bf16[1,1408,2048]{2,1,0:T(8,128)(2,1)} %param.19, f32[2,512,1408]{2,1,0:T(8,128)} %fusion.22, bf16[2,512,2048]{2,1,0:T(8,128)(2,1)} %bitcast.222, bf16[1,2048,1408]{2,1,0:T(8,128)(2,1)} %param.17), kind=kOutput, calls=%fused_computation.36 | convolution fusion | flops 11821907968 | bytes 25690112 | tf_op jit(solution)/shard_map/btf,fh->bth/dot_general | solution.py:66
  425.7 4.9 copy.70
  430.5 3.9 all-to-all-start.1
  434.4 0.1 reduce_sum.40
  434.6 0.1 copy.64
  434.7 51.6 %all-to-all-done.1 = bf16[2,32,16,2048]{3,2,0,1:T(8,128)(2,1)} async-done(((bf16[2,32,16,2048]{3,2,0,1:T(8,128)(2,1)}), bf16[2,32,16,2048]{3,2,0,1:T(8,128)(2,1)}, u32[]{:S(2)}, u32[]{:S(2)}) %all-to-all-start.1) | async-done | bytes 4194336 | tf_op jit(solution)/shard_map/all_to_all | solution.py:67
  486.3 4.8 copy.71
  491.0 12.9 %gather_fusion.1 = bf16[512,2048]{1,0:T(8,128)(2,1)} fusion(bf16[2,512,2048]{2,1,0:T(8,128)(2,1)} %bitcast.216, s32[512]{0:T(512)S(1)} %bitcast.218), kind=kCustom, calls=%fused_computation.1 | custom fusion | bytes 4198400 | tf_op jit(solution)/shard_map/vmap(jit(_take))/gather | solution.py:8
  504.0 4.4 gather.15
  508.4 2.9 copy_select_fusion.1
  511.3 1.6 fusion.33
  (48 shorter events, 0.5 us)
Async XLA Ops:
  6.5 200.5 %copy-start = (bf16[2,128,2048]{2,1,0:T(8,128)(2,1)S(1)}, bf16[2,128,2048]{2,1,0:T(8,128)(2,1)}, u32[]{:S(2)}) copy-start(bf16[2,128,2048]{2,1,0:T(8,128)(2,1)} %param.16) | copy-start | bytes 3145732
  6.6 53.7 %all-gather.4.cloned.1.call-start = ((), (), s32[]{:S(2)}) async-start(), calls=%async_computation.3 | async-start | bytes 9437184 | tf_op jit(solution)/shard_map/all_gather | solution.py:20
  7.3 105.3 %all-gather.8.cloned.1.call-start = ((), (), s32[]{:S(2)}) async-start(), calls=%async_computation.5 | async-start | bytes 5242880 | tf_op jit(solution)/shard_map/all_gather | solution.py:25
  67.3 104.4 %all-gather.6.cloned.1.call-start = ((), (), s32[]{:S(2)}) async-start(), calls=%async_computation.4 | async-start | bytes 5242880 | tf_op jit(solution)/shard_map/all_gather | solution.py:26
  78.1 227.9 %reduce-scatter.2.cloned.1.call-start = ((), (), s32[]{:S(2)}) async-start(), calls=%async_computation.6 | async-start | bytes 18874368 | tf_op jit(solution)/shard_map/reduce_scatter | solution.py:46
  112.6 15.7 %copy-start.8 = (bf16[2,1024,2,1,128]{4,1,2,0,3:T(8,128)(2,1)S(1)}, bf16[2,1024,2,1,128]{4,1,2,0,3:T(8,128)(2,1)}, u32[]{:S(2)}) copy-start(bf16[2,1024,2,1,128]{4,1,2,0,3:T(8,128)(2,1)} %fusion.43) | copy-start | bytes 3145732
  128.3 15.9 %copy-start.3 = (pred[512,4096]{0,1:T(8,128)(4,1)S(1)}, pred[512,4096]{0,1:T(8,128)(4,1)}, u32[]{:S(2)}) copy-start(pred[512,4096]{0,1:T(8,128)(4,1)} %get-tuple-element.6) | copy-start | bytes 6291460
  144.1 20.3 %copy-start.2 = (f32[2,2,4096,512]{3,2,1,0:T(8,128)S(1)}, f32[2,2,4096,512]{3,2,1,0:T(8,128)}, u32[]{:S(2)}) copy-start(f32[2,2,4096,512]{3,2,1,0:T(8,128)} %get-tuple-element.14) | copy-start | bytes 100663296
  216.4 0.7 copy-start.6
  217.1 89.0 %copy-start.5 = (bf16[2,128,2048]{2,1,0:T(8,128)(2,1)S(1)}, bf16[2,128,2048]{2,1,0:T(8,128)(2,1)}, u32[]{:S(2)}) copy-start(bf16[2,128,2048]{2,1,0:T(8,128)(2,1)} %param.10) | copy-start | bytes 3145732
  332.6 63.7 %slice-start = ((s8[5767168]{0:T(1024)(128)(4,1)}), s8[4194304]{0:T(1024)(128)(4,1)S(1)}, s32[]{:S(2)}) async-start(s8[5767168]{0:T(1024)(128)(4,1)} %bitcast.230), calls=%async_computation.7 | async-start | bytes 8388608
  393.7 2.7 slice-start.1
  394.3 2.1 copy-start.4
  430.5 4.2 copy-start.7
  430.5 55.7 %all-to-all-start.1 = ((bf16[2,32,16,2048]{3,2,0,1:T(8,128)(2,1)}), bf16[2,32,16,2048]{3,2,0,1:T(8,128)(2,1)}, u32[]{:S(2)}, u32[]{:S(2)}) async-start(bf16[2,32,16,2048]{3,2,0,1:T(8,128)(2,1)} %copy.70), calls=%async_computation.2 | async-start | bytes 8388608 | tf_op jit(solution)/shard_map/all_to_all | solution.py:67
  491.0 21.9 %copy-start.1 = (bf16[2,128,2048]{2,1,0:T(8,128)(2,1)S(1)}, bf16[2,128,2048]{2,1,0:T(8,128)(2,1)}, u32[]{:S(2)}) copy-start(bf16[2,128,2048]{2,1,0:T(8,128)(2,1)} %param.16) | copy-start | bytes 3145732
Sparse Core Ops, SparseCore 0:
  8.9 51.2 all-gather.3
  67.4 45.1 all-gather.7
  114.2 45.9 all-gather.5
  216.6 89.4 reduce-scatter.1
where the time goes:
time: 529 us; the launch traced here: 520 us
  waiting for transfers between devices  194 us (37%)
  matrix products  126 us (24%)
  local copies, waits for them, and re-layouts  83.5 us (16%)
  blocking collectives  61 us (12%)
  other arithmetic  36.3 us (7%)
  between operations  13.7 us (3%)
    reduce_scatter x1, waiting for transfers between devices, attend_local(): attn_sum = lax.psum_scatter(partial, 'tp', scatter_dimension=1, tiled=True)  61.9 us
    all_to_all x1, blocking collectives, dispatch_experts(): recv_buf = lax.all_to_all(send_buf, ('cp', 'tp'), 1, 1, tiled=True)  61 us
    all_gather x1, waiting for transfers between devices, attend_local(): x_half = lax.all_gather(act_in, 'tp', axis=1, tiled=True)  52.9 us
    all_to_all x1, waiting for transfers between devices, dispatch_experts(): lax.all_to_all(expert_out.reshape(n_micro, experts, capacity, hidden), ('...  51.6 us
    gather x3, local copies, waits for them, and re-layouts, pick_rows(): return jnp.take(row_table, row_ids, axis=0, mode='fill', fill_value=0)  39.6 us
    dot_general x2, matrix products, attend_local(): jnp.einsum('bhgqk,bkhd->bqhgd', exp_scores.astype(jnp.bfloat16), value_al...  35.3 us
    dot_general x2, matrix products, attend_local(): jnp.einsum('bqhgd,bkhd->bhgqk', q_part, key_all, preferred_element_type=j...  31.5 us
    all_gather x1, waiting for transfers between devices, attend_local(): key_all = lax.all_gather(key_half, 'cp', axis=1, tiled=True)  27 us
  transfers between devices with their start and end apart: 5, of which 4 were waited for; matrix products, arithmetic and copies ran while one was open for 19% of the time, Pallas kernels for 0%

commit v1 on v0

v1 whole, which is shorter than its diff:
```python
import functools

import jax
import jax.numpy as jnp
from jax import lax
from jax.experimental import pallas as pl
from jax.experimental.pallas import tpu as pltpu
from jax.sharding import PartitionSpec as P

LOG2E = 1.4426950408889634


def attention_body(pieces, piece_len, head_dim, qkv_ref, o_ref, s_ref):
    p = pl.program_id(0)
    half = pieces // 2
    factor = head_dim ** -0.5 * LOG2E

    def offset(n):
        return pl.multiple_of(jnp.where(n < half, 2 * piece_len * n, 2 * piece_len * (pieces - 1 - n) + piece_len), piece_len)

    q_rows = qkv_ref[pl.ds(offset(p), piece_len), 0:head_dim]

    def scores(n):
        k_rows = qkv_ref[pl.ds(offset(n), piece_len), head_dim:2 * head_dim]
        return lax.dot_general(q_rows, k_rows, (((1,), (1,)), ((), ())), preferred_element_type=jnp.float32)

    def fold(op, wide):
        parts = [wide[:, i * 128:(i + 1) * 128] for i in range(piece_len // 128)]
        while len(parts) > 1:
            parts = [op(a, b) for a, b in zip(parts[::2], parts[1::2])]
        return parts[0]

    def first(n, peak):
        s = scores(n)
        s_ref[n] = s
        return jnp.maximum(peak, fold(jnp.maximum, s))

    row = lax.broadcasted_iota(jnp.int32, (piece_len, piece_len), 0)
    col = lax.broadcasted_iota(jnp.int32, (piece_len, piece_len), 1)
    s_diag = jnp.where(col <= row, scores(p), -jnp.inf)
    s_ref[p] = s_diag
    peak = lax.fori_loop(0, p, first, fold(jnp.maximum, s_diag))
    peak = jnp.max(peak, axis=1, keepdims=True) * factor

    def second(n, carry):
        total, acc = carry
        e = jnp.exp2(s_ref[n] * factor - peak)
        v_rows = qkv_ref[pl.ds(offset(n), piece_len), 2 * head_dim:3 * head_dim]
        acc = acc + jnp.dot(e.astype(jnp.bfloat16), v_rows, preferred_element_type=jnp.float32)
        return total + fold(jnp.add, e), acc

    zero = jnp.zeros((piece_len, 128), jnp.float32)
    total, acc = lax.fori_loop(0, p + 1, second, (zero, jnp.zeros((piece_len, head_dim), jnp.float32)))
    total = jnp.sum(total, axis=1, keepdims=True)
    o_ref[pl.ds(offset(p), piece_len), :] = (acc / total).astype(jnp.bfloat16)


def attend_unit(qkv, pieces):
    rows, width = qkv.shape
    head_dim = width // 3
    piece_len = rows // pieces
    return pl.pallas_call(
        functools.partial(attention_body, pieces, piece_len, head_dim),
        grid=(pieces,),
        out_shape=jax.ShapeDtypeStruct((rows, head_dim), jnp.bfloat16),
        in_specs=[pl.BlockSpec((rows, width), lambda p: (0, 0))],
        out_specs=pl.BlockSpec((rows, head_dim), lambda p: (0, 0)),
        scratch_shapes=[pltpu.VMEM((pieces, piece_len, piece_len), jnp.float32)],
        compiler_params=pltpu.CompilerParams(vmem_limit_bytes=40 << 20),
        cost_estimate=pl.CostEstimate(flops=9 * 4 * rows * rows * head_dim // 16, bytes_accessed=4 * rows * head_dim * 2, transcendentals=0),
    )(qkv)


def solution(mesh):
    cp_size = mesh.shape['cp']
    tp_size = mesh.shape['tp']
    experts = cp_size * tp_size
    row_spec = P(None, ('data', 'cp', 'tp'), None)
    head_spec = P(None, 'tp', None)
    out_spec = P('tp', None, None)
    expert_spec = P(('cp', 'tp'), None, None)

    def device_step(act_in, route_ids, route_gates, w_query, w_key, w_value, w_out, w_gate, w_up, w_down):
        n_micro, tokens, hidden = act_in.shape
        heads, head_dim = w_query.shape[1], w_query.shape[2]
        half_rows = tokens * tp_size
        w_qkv = jnp.concatenate([w_query, w_key, w_value], axis=2)
        x_half = lax.all_gather(act_in, 'tp', axis=1, tiled=True)
        w_full = lax.all_gather(w_out, 'tp', axis=0, tiled=True)
        qkv = jnp.einsum('bsh,hnd->bnsd', x_half, w_qkv, preferred_element_type=jnp.float32).astype(jnp.bfloat16)
        unit = lax.all_to_all(qkv.reshape(n_micro * heads, half_rows, 3 * head_dim), 'cp', 0, 0, tiled=True)
        o_unit = attend_unit(unit.reshape(cp_size * half_rows, 3 * head_dim), 2 * cp_size)
        o_recv = lax.all_to_all(o_unit.reshape(experts, tokens, head_dim), ('cp', 'tp'), 0, 0, tiled=True)
        o_rows = o_recv.reshape(n_micro, heads, tp_size, tokens, head_dim).transpose(0, 3, 2, 1, 4).reshape(n_micro, tokens, tp_size * heads * head_dim)
        attn = jnp.einsum('bsk,kh->bsh', o_rows, w_full.reshape(tp_size * heads * head_dim, hidden), preferred_element_type=jnp.float32)
        mid_rows = (act_in.astype(jnp.float32) + attn).astype(jnp.bfloat16)

        capacity = (4 * tokens) // experts
        slots = experts * capacity
        flat_ids = route_ids.reshape(n_micro, 2 * tokens)
        hits = (flat_ids[..., None] == jnp.arange(experts)).astype(jnp.bfloat16)
        before = (jnp.arange(2 * tokens)[:, None] > jnp.arange(2 * tokens)[None, :]).astype(jnp.bfloat16)
        rank = jnp.einsum('ij,bje->bie', before, hits, preferred_element_type=jnp.float32)
        slot_rank = jnp.sum(rank * hits.astype(jnp.float32), axis=-1).astype(jnp.int32)
        dest_slot = (flat_ids * capacity + slot_rank).reshape(n_micro, tokens, 2)
        slot_ix = jnp.arange(slots)
        pick0 = (dest_slot[:, :, 0:1] == slot_ix).astype(jnp.bfloat16)
        pick1 = (dest_slot[:, :, 1:2] == slot_ix).astype(jnp.bfloat16)
        send_buf = jnp.einsum('bts,bth->bsh', pick0 + pick1, mid_rows, preferred_element_type=jnp.float32).astype(jnp.bfloat16)
        recv_buf = lax.all_to_all(send_buf.reshape(n_micro, experts, capacity, hidden), ('cp', 'tp'), 1, 1, tiled=True)
        expert_in = recv_buf.reshape(n_micro, slots, hidden)
        gate_act = jnp.einsum('bth,hf->btf', expert_in, w_gate[0], preferred_element_type=jnp.float32)
        up_act = jnp.einsum('bth,hf->btf', expert_in, w_up[0], preferred_element_type=jnp.float32)
        mixed_act = (jax.nn.silu(gate_act) * up_act).astype(jnp.bfloat16)
        expert_out = jnp.einsum('btf,fh->bth', mixed_act, w_down[0], preferred_element_type=jnp.float32).astype(jnp.bfloat16)
        back = lax.all_to_all(expert_out.reshape(n_micro, experts, capacity, hidden), ('cp', 'tp'), 1, 1, tiled=True).reshape(n_micro, slots, hidden)
        z0 = jnp.einsum('bts,bsh->bth', pick0, back, preferred_element_type=jnp.float32)
        z1 = jnp.einsum('bts,bsh->bth', pick1, back, preferred_element_type=jnp.float32)
        combined = route_gates[:, :, 0:1] * z0 + route_gates[:, :, 1:2] * z1
        return (mid_rows.astype(jnp.float32) + combined).astype(jnp.bfloat16)

    return jax.shard_map(device_step, mesh=mesh, in_specs=(row_spec, row_spec, row_spec, head_spec, head_spec, head_spec, out_spec, expert_spec, expert_spec, expert_spec), out_specs=row_spec, check_vma=False)
```

time: 529 us -> 345 us (0.65)
  waiting for transfers between devices: 194 us -> 116 us
  matrix products: 126 us -> 51.7 us
  local copies, waits for them, and re-layouts: 83.5 us -> 22.3 us
  blocking collectives: 61 us -> 98 us
  other arithmetic: 36.3 us -> 0.01 us
  Pallas kernels: 0 us -> 28.9 us
  starting transfers between devices: 4.54 us -> 10.2 us
    dot_general x10 -> x8, matrix products: 126 us -> 51.7 us  [the longest x1 20.9 us: device_step(): jnp.einsum('btf,fh->bth', mixed_act, w_down[0], preferred_element_type=jn...]
    reduce_scatter x1 -> x0, waiting for transfers between devices: 61.9 us -> none  [attend_local(): attn_sum = lax.psum_scatter(partial, 'tp', scatter_dimension=1, tiled=True)]
    gather x3 -> x0, local copies, waits for them, and re-layouts: 39.6 us -> none  [pick_rows(): return jnp.take(row_table, row_ids, axis=0, mode='fill', fill_value=0)]
    all_to_all x1 -> x2, blocking collectives: 61 us -> 98 us  [the longest x1 57.1 us: device_step(): lax.all_to_all(send_buf.reshape(n_micro, experts, capacity, hidden), ('cp...]
    all_gather x3 -> x2, waiting for transfers between devices: 79.9 us -> 46.9 us  [the longest x1 46.9 us: device_step(): x_half = lax.all_gather(act_in, 'tp', axis=1, tiled=True)]
    pallas_call x0 -> x1, Pallas kernels: none -> 28.9 us  [attend_unit(): pl.pallas_call(functools.partial(attention_body, pieces, piece_len, head_...]
    scatter x1 -> x0, local copies, waits for them, and re-layouts: 24.5 us -> none  [dispatch_experts(): jnp.full((n_micro, experts * capacity), tokens, jnp.int32)]
    reduce_sum x3 -> x0, other arithmetic: 22.5 us -> none  [the longest x2 22.4 us: attend_local(): row_sum = jnp.sum(exp_scores, axis=-1)]
  transfers between devices with their start and end apart: 5 -> 4, of which waited for: 4 -> 3; matrix products, arithmetic and copies ran while one was open for 19% -> 7% of each run, Pallas kernels for 0% -> 9%
where the time goes in v1:
time: 345 us; the launch traced here: 340 us
  waiting for transfers between devices  116 us (34%)
  blocking collectives  98 us (28%)
  matrix products  51.7 us (15%)
  Pallas kernels  28.9 us (8%)
  local copies, waits for them, and re-layouts  22.3 us (6%)
  between operations  13.6 us (4%)
  starting transfers between devices  10.2 us (3%)
    all_to_all x1, blocking collectives, device_step(): lax.all_to_all(send_buf.reshape(n_micro, experts, capacity, hidden), ('cp...  57.1 us
    all_to_all x1, waiting for transfers between devices, device_step(): lax.all_to_all(expert_out.reshape(n_micro, experts, capacity, hidden), ('...  51.5 us
    all_gather x1, waiting for transfers between devices, device_step(): x_half = lax.all_gather(act_in, 'tp', axis=1, tiled=True)  46.9 us
    all_to_all x1, blocking collectives, device_step(): lax.all_to_all(qkv.reshape(n_micro * heads, half_rows, 3 * head_dim), 'cp...  40.9 us
    pallas_call x1, Pallas kernels, attend_unit(): pl.pallas_call(functools.partial(attention_body, pieces, piece_len, head_...  28.9 us
    dot_general x1, matrix products, device_step(): jnp.einsum('btf,fh->bth', mixed_act, w_down[0], preferred_element_type=jn...  20.9 us
    all_to_all x1, waiting for transfers between devices, device_step(): lax.all_to_all(o_unit.reshape(experts, tokens, head_dim), ('cp', 'tp'), 0...  15.7 us
    dot_general x1, matrix products, device_step(): jnp.einsum('bsh,hnd->bnsd', x_half, w_qkv, preferred_element_type=jnp.flo...  11.6 us
  transfers between devices with their start and end apart: 4, of which 3 were waited for; matrix products, arithmetic and copies ran while one was open for 7% of the time, Pallas kernels for 9%

profile of v1, /device:TPU:97, one launch (start us, length us, event | category | flops | bytes accessed | tf_op | source)
XLA Modules:
  0.0 340.3 jit_solution(17027218326700880622)
XLA Ops:
  6.5 0.0 copy-start.1
  6.5 0.0 copy-start.2
  6.6 0.0 all-gather.3.cloned.1.call-start
  6.6 0.7 all-gather.3.cloned.1.call-update
  7.3 0.1 all-gather.5.cloned.1.call-start
  7.4 0.7 all-gather.5.cloned.1.call-update
  8.1 2.4 copy.47
  10.6 0.0 copy-done.1
  10.6 2.0 copy.48
  12.6 0.0 copy-done.2
  12.6 0.8 copy.49
  13.4 46.9 %all-gather.3.cloned.1.call-done = bf16[2,1024,2048]{2,1,0:T(8,128)(2,1)} async-done(((bf16[2,128,2048]{2,1,0:T(8,128)(2,1)}), bf16[2,1024,2048]{2,1,0:T(8,128)(2,1)}) %all-gather.3.cloned.1.call-update) | async-done | bytes 8388624 | tf_op jit(solution)/shard_map/all_gather | solution.py:88
  60.2 11.6 %convert_bitcast_fusion = bf16[2,2,1024,384]{2,3,0,1:T(8,128)(2,1)} fusion(bf16[2,1024,2048]{2,1,0:T(8,128)(2,1)} %all-gather.3.cloned.1.call-done, bf16[2048,2,128]{0,2,1:T(8,128)(2,1)S(1)} %copy.49, bf16[2048,2,128]{0,2,1:T(8,128)(2,1)} %copy.48, bf16[2048,2,128]{0,2,1:T(8,128)(2,1)S(1)} %copy.47), kind=kOutput, calls=%fused_computation.16 | convolution fusion | flops 6453460992 | bytes 14680064 | tf_op jit(solution)/shard_map/bsh,hnd->bnsd/dot_general | solution.py:90
  71.8 3.4 %copy.50 = bf16[2,2,1024,384]{3,2,1,0:T(8,128)(2,1)S(1)} copy(bf16[2,2,1024,384]{2,3,0,1:T(8,128)(2,1)} %convert_bitcast_fusion) | data formatting | bytes 6291456 | tf_op jit(solution)/shard_map/convert_element_type | solution.py:90
  75.3 40.9 %all_to_all.20 = bf16[4,1024,384]{2,1,0:T(8,128)(2,1)S(1)} all-to-all(bf16[4,1024,384]{2,1,0:T(8,128)(2,1)S(1)} %bitcast.70), channel_id=1, replica_groups=mesh['data'=1,'cp'=4,'tp'=8] {'cp'}, dimensions={0} | all-to-all | bytes 6291456 | tf_op jit(solution)/shard_map/all_to_all | solution.py:91
  116.2 0.0 copy-start.4
  116.2 28.9 %shard_map.100 = bf16[4096,128]{1,0:T(8,128)(2,1)} custom-call(bf16[4096,384]{1,0:T(8,128)(2,1)S(1)} %bitcast.66), custom_call_target="tpu_custom_call" | custom-call | flops 4831838208 | bytes 4194304 | tf_op jit(solution)/shard_map/pallas_call | solution.py:62
  145.2 0.0 copy-start.3
  145.2 4.3 %all-to-all-start.1 = ((bf16[32,128,128]{2,1,0:T(8,128)(2,1)}), bf16[32,128,128]{2,1,0:T(8,128)(2,1)S(1)}, u32[]{:S(2)}, u32[]{:S(2)}) async-start(bf16[32,128,128]{2,1,0:T(8,128)(2,1)} %bitcast.6), calls=%async_computation.1 | async-start | bytes 2097152 | tf_op jit(solution)/shard_map/all_to_all | solution.py:93
  149.5 0.0 copy-done.4
  149.5 0.1 copy.52
  149.7 0.1 eq.45
  149.8 0.2 fusion.24
  150.0 0.1 convert_element_type.55
  150.2 0.1 copy.53
  150.3 15.7 %all-to-all-done.1 = bf16[32,128,128]{2,1,0:T(8,128)(2,1)S(1)} async-done(((bf16[32,128,128]{2,1,0:T(8,128)(2,1)}), bf16[32,128,128]{2,1,0:T(8,128)(2,1)S(1)}, u32[]{:S(2)}, u32[]{:S(2)}) %all-to-all-start.1) | async-done | bytes 1048608 | tf_op jit(solution)/shard_map/all_to_all | solution.py:93
  165.9 1.1 copy.62
  167.0 1.6 reshape.39
  168.6 0.0 copy-done.3
  168.6 6.1 %fusion.19 = bf16[2,128,2048]{2,1,0:T(8,128)(2,1)S(1)} fusion(bf16[2,128,2048]{2,1,0:T(8,128)(2,1)} %reshape.39, bf16[2048,2048,1]{1,0,2:T(8,128)(2,1)} %bitcast.82, bf16[2,128,2048]{2,1,0:T(8,128)(2,1)S(1)} %copy-done.3), kind=kOutput, calls=%fused_computation.22 | convolution fusion | flops 2149056512 | bytes 11534336 | tf_op jit(solution)/shard_map/bsk,kh->bsh/dot_general | solution.py:95
  174.7 1.4 convolution_convert_fusion
  176.1 0.6 copy.55
  176.6 0.0 slice-start
  176.7 57.1 %all_to_all.21 = bf16[2,32,16,2048]{3,2,0,1:T(8,128)(2,1)S(1)} all-to-all(bf16[2,32,16,2048]{3,2,0,1:T(8,128)(2,1)S(1)} %copy.55), channel_id=1, replica_groups=mesh['data'=1,'cp'=4,'tp'=8] {'cp','tp'}, dimensions={1} | all-to-all | bytes 8388608 | tf_op jit(solution)/shard_map/all_to_all | solution.py:110
  233.8 0.6 copy.56
  234.3 0.0 copy-start
  234.3 2.1 copy-done
  236.4 0.0 slice-done
  236.4 0.0 slice-done.1
  236.4 8.5 %fusion.4 = f32[2,512,1408]{2,1,0:T(8,128)} fusion(bf16[2,512,2048]{2,1,0:T(8,128)(2,1)S(1)} %bitcast.71, bf16[1,2048,1408]{2,1,0:T(8,128)(2,1)S(1)} %bitcast.84), kind=kOutput, calls=%fused_computation.4 | convolution fusion | flops 5905580032 | bytes 15728640 | tf_op jit(solution)/shard_map/bth,hf->btf/dot_general | solution.py:113
  244.9 20.9 %fusion.10 = bf16[2,512,2048]{2,1,0:T(8,128)(2,1)} fusion(bf16[1,1408,2048]{2,1,0:T(8,128)(2,1)} %param.19, f32[2,512,1408]{2,1,0:T(8,128)} %fusion.4, bf16[2,512,2048]{2,1,0:T(8,128)(2,1)} %bitcast.72, bf16[1,2048,1408]{2,1,0:T(8,128)(2,1)} %param.17), kind=kOutput, calls=%fused_computation.9 | convolution fusion | flops 11821907968 | bytes 25690112 | tf_op jit(solution)/shard_map/btf,fh->bth/dot_general | solution.py:115
  265.9 4.7 %copy.57 = bf16[2,32,16,2048]{3,2,0,1:T(8,128)(2,1)} copy(bf16[2,32,16,2048]{3,2,1,0:T(8,128)(2,1)} %bitcast.73) | data formatting | bytes 8388608 | tf_op jit(solution)/shard_map/reshape | solution.py:116
  270.6 5.8 %all-to-all-start.3 = ((bf16[2,32,16,2048]{3,2,0,1:T(8,128)(2,1)}), bf16[2,32,16,2048]{3,2,0,1:T(8,128)(2,1)}, u32[]{:S(2)}, u32[]{:S(2)}) async-start(bf16[2,32,16,2048]{3,2,0,1:T(8,128)(2,1)} %copy.57), calls=%async_computation.3 | async-start | bytes 8388608 | tf_op jit(solution)/shard_map/all_to_all | solution.py:116
  276.4 0.0 copy-done.5
  276.4 51.5 %all-to-all-done.3 = bf16[2,32,16,2048]{3,2,0,1:T(8,128)(2,1)} async-done(((bf16[2,32,16,2048]{3,2,0,1:T(8,128)(2,1)}), bf16[2,32,16,2048]{3,2,0,1:T(8,128)(2,1)}, u32[]{:S(2)}, u32[]{:S(2)}) %all-to-all-start.3) | async-done | bytes 4194336 | tf_op jit(solution)/shard_map/all_to_all | solution.py:116
  327.9 2.5 copy.58
  330.4 0.8 convolution_multiply_fusion
  331.2 2.2 fusion.20
  (8 shorter events, 0.0 us)
Async XLA Ops:
  6.5 4.0 %copy-start.1 = (bf16[2048,2,128]{2,1,0:T(2,128)(2,1)S(1)}, bf16[2048,2,128]{2,1,0:T(2,128)(2,1)}, u32[]{:S(2)}) copy-start(bf16[2048,2,128]{2,1,0:T(2,128)(2,1)} %param.14) | copy-start | bytes 3145732
  6.5 6.0 %copy-start.2 = (bf16[2048,2,128]{2,1,0:T(2,128)(2,1)S(1)}, bf16[2048,2,128]{2,1,0:T(2,128)(2,1)}, u32[]{:S(2)}) copy-start(bf16[2048,2,128]{2,1,0:T(2,128)(2,1)} %param.15) | copy-start | bytes 3145732
  6.6 53.7 %all-gather.3.cloned.1.call-start = ((), (), s32[]{:S(2)}) async-start(), calls=%async_computation.4 | async-start | bytes 9437184 | tf_op jit(solution)/shard_map/all_gather | solution.py:88
  7.3 161.3 %all-gather.5.cloned.1.call-start = ((), (), s32[]{:S(2)}) async-start(), calls=%async_computation.5 | async-start | bytes 9437184 | tf_op jit(solution)/shard_map/all_gather | solution.py:89
  116.2 33.3 %copy-start.4 = (s32[2,128,2]{1,2,0:T(2,128)S(1)}, s32[2,128,2]{1,2,0:T(2,128)}, u32[]{:S(2)}) copy-start(s32[2,128,2]{1,2,0:T(2,128)} %param.11) | copy-start | bytes 6148
  145.2 23.5 %copy-start.3 = (bf16[2,128,2048]{2,1,0:T(8,128)(2,1)S(1)}, bf16[2,128,2048]{2,1,0:T(8,128)(2,1)}, u32[]{:S(2)}) copy-start(bf16[2,128,2048]{2,1,0:T(8,128)(2,1)} %param.10) | copy-start | bytes 3145732
  145.2 20.8 %all-to-all-start.1 = ((bf16[32,128,128]{2,1,0:T(8,128)(2,1)}), bf16[32,128,128]{2,1,0:T(8,128)(2,1)S(1)}, u32[]{:S(2)}, u32[]{:S(2)}) async-start(bf16[32,128,128]{2,1,0:T(8,128)(2,1)} %bitcast.6), calls=%async_computation.1 | async-start | bytes 2097152 | tf_op jit(solution)/shard_map/all_to_all | solution.py:93
  176.6 59.8 %slice-start = ((s8[5767168]{0:T(1024)(128)(4,1)}), s8[4194304]{0:T(1024)(128)(4,1)S(1)}, s32[]{:S(2)}) async-start(s8[5767168]{0:T(1024)(128)(4,1)} %bitcast.83), calls=%async_computation.6 | async-start | bytes 8388608
  233.7 2.7 slice-start.1
  234.3 2.1 copy-start
  270.6 5.8 %copy-start.5 = (f32[2,128,2]{1,2,0:T(2,128)S(1)}, f32[2,128,2]{1,2,0:T(2,128)}, u32[]{:S(2)}) copy-start(f32[2,128,2]{1,2,0:T(2,128)} %param.12) | copy-start | bytes 6148
  270.6 57.3 %all-to-all-start.3 = ((bf16[2,32,16,2048]{3,2,0,1:T(8,128)(2,1)}), bf16[2,32,16,2048]{3,2,0,1:T(8,128)(2,1)}, u32[]{:S(2)}, u32[]{:S(2)}) async-start(bf16[2,32,16,2048]{3,2,0,1:T(8,128)(2,1)} %copy.57), calls=%async_computation.3 | async-start | bytes 8388608 | tf_op jit(solution)/shard_map/all_to_all | solution.py:116
Sparse Core Ops, SparseCore 0:
  8.9 51.2 all-gather.2
  61.9 47.1 all-gather.4

commit v2 on v1

--- a/solution.py
+++ b/solution.py
@@ -71,6 +71,204 @@
     )(qkv)
 
 
+MESH_ID = pl.DeviceIdType.MESH
+
+
+def expert_body(cp, tp, h_ref, sel_ref, pick_ref, g_ref, wg_hbm, wu_hbm, wd_hbm, y_ref,
+                s0, s1, r0, r1, e0, e1, z0, z1, b0, b1, f0, f1, wg, wu, wd, rows_in, act, w_sem,
+                out_x, out_y, mid_y, mid_x, ret_y, ret_x, fin_x, fin_y):
+    d, c, t = lax.axis_index('data'), lax.axis_index('cp'), lax.axis_index('tp')
+    cap, hidden = s0.shape[2], s0.shape[3]
+    ff = wg.shape[1]
+    nx = tp // 2
+    ring = sorted(range(cp), key=lambda i: min(i, cp - i))
+    x, k = t // 2, t % 2
+
+    def tp_at(dx, dk):
+        return ((x + dx) % nx) * 2 + (k + dk) % 2
+
+    def tp_from(dx, dk):
+        return ((x + nx - dx) % nx) * 2 + (k + dk) % 2
+
+    def cp_at(dc):
+        return (c + dc) % cp
+
+    def cp_from(dc):
+        return (c + cp - dc) % cp
+
+    near = [(0, 1)] + [(dx, dk) for dx in ring[1:] for dk in (0, 1)]
+    cols = ring[1:]
+
+    weights = [pltpu.make_async_copy(a, b, w_sem.at[i]) for i, (a, b) in enumerate(((wg_hbm, wg), (wu_hbm, wu), (wd_hbm, wd)))]
+    for copy in weights:
+        copy.start()
+
+    barrier = pltpu.get_barrier_semaphore()
+    for dx, dk in near:
+        pl.semaphore_signal(barrier, inc=1, device_id=(d, c, tp_at(dx, dk)), device_id_type=MESH_ID)
+    for dc in cols:
+        pl.semaphore_signal(barrier, inc=1, device_id=(d, cp_at(dc), t), device_id_type=MESH_ID)
+
+    def send(src, dst, sems, key, cc, tt):
+        return pltpu.make_async_remote_copy(src_ref=src, dst_ref=dst, send_sem=sems.at[(0,) + key], recv_sem=sems.at[(1,) + key], device_id=(d, cc, tt), device_id_type=MESH_ID)
+
+    def select(b, buf):
+        tile = 256
+
+        @pl.loop(0, hidden // tile)
+        def _(n):
+            at = pl.ds(pl.multiple_of(n * tile, tile), tile)
+            got = jnp.dot(sel_ref[b], h_ref[b, :, at], preferred_element_type=jnp.float32).astype(jnp.bfloat16)
+            buf[:, :, :, at] = got.reshape(buf.shape[:3] + (tile,))
+
+    select(0, s0)
+    pl.semaphore_wait(barrier, len(near) + len(cols))
+    first_x = {}
+    for dx, dk in near:
+        tt = tp_at(dx, dk)
+        first_x[dx, dk] = send(s0.at[tt], r0.at[:, t], out_x, (dx, dk), c, tt)
+        first_x[dx, dk].start()
+    select(1, s1)
+    first_y = {}
+    for dc in cols:
+        cc = cp_at(dc)
+        first_y[dc] = send(s1.at[cc], r1.at[:, c], out_y, (dc,), cc, t)
+        first_y[dc].start()
+    r0[:, pl.ds(t, 1)] = s0[t][:, None]
+    r1[:, pl.ds(c, 1)] = s1[c][:, None]
+
+    for key in near:
+        first_x[key].wait_recv()
+    second_y = {}
+    for dc in cols:
+        cc = cp_at(dc)
+        second_y[dc] = send(r0.at[cc], e0.at[c], mid_y, (dc,), cc, t)
+        second_y[dc].start()
+    for dc in cols:
+        first_y[dc].wait_recv()
+    second_x = {}
+    for dx, dk in near:
+        tt = tp_at(dx, dk)
+        second_x[dx, dk] = send(r1.at[tt], e1.at[t], mid_x, (dx, dk), c, tt)
+        second_x[dx, dk].start()
+    for copy in weights:
+        copy.wait()
+
+    seg = tp * cap
+    sub = cp * cap
+
+    def run_expert():
+        @pl.loop(0, ff // 128)
+        def _(n):
+            at = pl.ds(pl.multiple_of(n * 128, 128), 128)
+            both = jnp.dot(rows_in[...], jnp.concatenate([wg[:, at], wu[:, at]], axis=1), preferred_element_type=jnp.float32)
+            gate, up = both[:, :128], both[:, 128:]
+            act[:, at] = (jax.nn.silu(gate) * up).astype(jnp.bfloat16)
+
+        @pl.loop(0, hidden // 256)
+        def _(n):
+            at = pl.ds(pl.multiple_of(n * 256, 256), 256)
+            rows_in[:, at] = jnp.dot(act[...], wd[:, at], preferred_element_type=jnp.float32).astype(jnp.bfloat16)
+
+    back_y, back_x, last_x, last_y = {}, {}, {}, {}
+
+    def forward(step):
+        dc = dx = ring[step]
+        if step:
+            back_y[dc].wait_recv()
+            back_x[dx, 0].wait_recv()
+        back_x[dx, 1].wait_recv()
+        ce = cp_at(dc)
+        for tx, tk in near:
+            tt = tp_at(tx, tk)
+            last_x[dc, tx, tk] = send(b0.at[tt, ce], f0.at[t, ce], fin_x, (dc, tx, tk), c, tt)
+            last_x[dc, tx, tk].start()
+        pair = pl.ds(((x + dx) % nx) * 2, 2)
+        for tc in cols:
+            cc = cp_at(tc)
+            last_y[dx, tc] = send(b1.at[cc, pair], f1.at[c, pair], fin_y, (dx, tc), cc, t)
+            last_y[dx, tc].start()
+        f0[t, pl.ds(ce, 1)] = b0[t, pl.ds(ce, 1)]
+        f1[c, pair] = b1[c, pair]
+
+    for step in range(cp):
+        dc = dx = ring[step]
+        if step == 0:
+            second_x[0, 1].wait_recv()
+            rows_in[0:seg] = r0[c].reshape(seg, hidden)
+            rows_in[seg:seg + sub] = r1[t].reshape(sub, hidden)
+            rows_in[seg + sub:seg + 2 * sub] = e1[tp_from(0, 1)].reshape(sub, hidden)
+        else:
+            second_y[dc].wait_recv()
+            second_x[dx, 0].wait_recv()
+            second_x[dx, 1].wait_recv()
+            rows_in[0:seg] = e0[cp_from(dc)].reshape(seg, hidden)
+            rows_in[seg:seg + sub] = e1[tp_from(dx, 0)].reshape(sub, hidden)
+            rows_in[seg + sub:seg + 2 * sub] = e1[tp_from(dx, 1)].reshape(sub, hidden)
+        run_expert()
+        if step == 0:
+            b0[:, pl.ds(c, 1)] = rows_in[0:seg].reshape(tp, 1, cap, hidden)
+            b1[:, pl.ds(t, 1)] = rows_in[seg:seg + sub].reshape(cp, 1, cap, hidden)
+        else:
+            cs = cp_from(dc)
+            z0[cs] = rows_in[0:seg].reshape(tp, cap, hidden)
+            back_y[dc] = send(z0.at[cs], b0.at[:, c], ret_y, (dc,), cs, t)
+            back_y[dc].start()
+            ts = tp_from(dx, 0)
+            z1[ts] = rows_in[seg:seg + sub].reshape(cp, cap, hidden)
+            back_x[dx, 0] = send(z1.at[ts], b1.at[:, t], ret_x, (dx, 0), c, ts)
+            back_x[dx, 0].start()
+        ts = tp_from(dx, 1)
+        z1[ts] = rows_in[seg + sub:seg + 2 * sub].reshape(cp, cap, hidden)
+        back_x[dx, 1] = send(z1.at[ts], b1.at[:, t], ret_x, (dx, 1), c, ts)
+        back_x[dx, 1].start()
+        if step == 1:
+            forward(0)
+    for step in range(1, cp):
+        forward(step)
+    for copy in list(last_x.values()) + list(last_y.values()):
+        copy.wait_recv()
+
+    tokens = h_ref.shape[1]
+    slots = cp * tp * cap
+
+    @pl.loop(0, hidden // 256)
+    def _(n):
+        at = pl.ds(pl.multiple_of(n * 256, 256), 256)
+        for b, buf in enumerate((f0, f1)):
+            got = jnp.dot(pick_ref[b], buf[:, :, :, at].reshape(slots, 256), preferred_element_type=jnp.float32)
+            mixed = g_ref[b, :, 0:1] * got[:tokens] + g_ref[b, :, 1:2] * got[tokens:]
+            y_ref[b, :, at] = (h_ref[b, :, at].astype(jnp.float32) + mixed).astype(jnp.bfloat16)
+
+    for group in (first_x, first_y, second_x, second_y, back_x, back_y, last_x, last_y):
+        for copy in group.values():
+            copy.wait_send()
+
+
+def run_experts(mid_rows, sel, pick, route_gates, w_gate, w_up, w_down, cp, tp, cap):
+    n_micro, tokens, hidden = mid_rows.shape
+    ff = w_gate.shape[1]
+    bf16 = jnp.bfloat16
+    by_x, by_y = (tp, cp, cap, hidden), (cp, tp, cap, hidden)
+    rows = 2 * (tp * cap)
+    nx = tp // 2
+    vmem = pl.BlockSpec(memory_space=pltpu.VMEM)
+    any_spec = pl.BlockSpec(memory_space=pl.ANY)
+    dma = pltpu.SemaphoreType.DMA
+    return pl.pallas_call(
+        functools.partial(expert_body, cp, tp),
+        out_shape=jax.ShapeDtypeStruct(mid_rows.shape, bf16),
+        in_specs=[vmem] * 4 + [any_spec] * 3,
+        out_specs=vmem,
+        scratch_shapes=[pltpu.VMEM(s, bf16) for s in (by_x, by_y, by_y, by_x, by_y, by_x, by_y, by_x, by_x, by_y, by_x, by_y)]
+        + [pltpu.VMEM((hidden, ff), bf16), pltpu.VMEM((hidden, ff), bf16), pltpu.VMEM((ff, hidden), bf16)]
+        + [pltpu.VMEM((rows, hidden), bf16), pltpu.VMEM((rows, ff), bf16)]
+        + [dma((3,)), dma((2, nx, 2)), dma((2, cp)), dma((2, cp)), dma((2, nx, 2)), dma((2, cp)), dma((2, nx, 2)), dma((2, cp, nx, 2)), dma((2, nx, cp))],
+        compiler_params=pltpu.CompilerParams(collective_id=1, has_side_effects=True, vmem_limit_bytes=60 << 20),
+        cost_estimate=pl.CostEstimate(flops=6 * 4 * rows * hidden * ff, bytes_accessed=6 * hidden * ff, transcendentals=0),
+    )(mid_rows, sel, pick, route_gates, w_gate, w_up, w_down)
+
+
 def solution(mesh):
     cp_size = mesh.shape['cp']
     tp_size = mesh.shape['tp']
@@ -102,21 +300,12 @@
         before = (jnp.arange(2 * tokens)[:, None] > jnp.arange(2 * tokens)[None, :]).astype(jnp.bfloat16)
         rank = jnp.einsum('ij,bje->bie', before, hits, preferred_element_type=jnp.float32)
         slot_rank = jnp.sum(rank * hits.astype(jnp.float32), axis=-1).astype(jnp.int32)
-        dest_slot = (flat_ids * capacity + slot_rank).reshape(n_micro, tokens, 2)
+        chip_slot = (flat_ids % tp_size * cp_size + flat_ids // tp_size) * capacity
+        base_slot = jnp.where(jnp.arange(n_micro)[:, None] == 0, chip_slot, flat_ids * capacity)
+        dest_slot = (base_slot + slot_rank).reshape(n_micro, tokens, 2).transpose(0, 2, 1).reshape(n_micro, 2 * tokens)
         slot_ix = jnp.arange(slots)
-        pick0 = (dest_slot[:, :, 0:1] == slot_ix).astype(jnp.bfloat16)
-        pick1 = (dest_slot[:, :, 1:2] == slot_ix).astype(jnp.bfloat16)
-        send_buf = jnp.einsum('bts,bth->bsh', pick0 + pick1, mid_rows, preferred_element_type=jnp.float32).astype(jnp.bfloat16)
-        recv_buf = lax.all_to_all(send_buf.reshape(n_micro, experts, capacity, hidden), ('cp', 'tp'), 1, 1, tiled=True)
-        expert_in = recv_buf.reshape(n_micro, slots, hidden)
-        gate_act = jnp.einsum('bth,hf->btf', expert_in, w_gate[0], preferred_element_type=jnp.float32)
-        up_act = jnp.einsum('bth,hf->btf', expert_in, w_up[0], preferred_element_type=jnp.float32)
-        mixed_act = (jax.nn.silu(gate_act) * up_act).astype(jnp.bfloat16)
-        expert_out = jnp.einsum('btf,fh->bth', mixed_act, w_down[0], preferred_element_type=jnp.float32).astype(jnp.bfloat16)
-        back = lax.all_to_all(expert_out.reshape(n_micro, experts, capacity, hidden), ('cp', 'tp'), 1, 1, tiled=True).reshape(n_micro, slots, hidden)
-        z0 = jnp.einsum('bts,bsh->bth', pick0, back, preferred_element_type=jnp.float32)
-        z1 = jnp.einsum('bts,bsh->bth', pick1, back, preferred_element_type=jnp.float32)
-        combined = route_gates[:, :, 0:1] * z0 + route_gates[:, :, 1:2] * z1
-        return (mid_rows.astype(jnp.float32) + combined).astype(jnp.bfloat16)
+        pick = (dest_slot[:, :, None] == slot_ix).astype(jnp.bfloat16)
+        sel = jnp.any((dest_slot[:, None, :] == slot_ix[:, None]).reshape(n_micro, slots, 2, tokens), axis=2).astype(jnp.bfloat16)
+        return run_experts(mid_rows, sel, pick, route_gates, w_gate[0], w_up[0], w_down[0], cp_size, tp_size, capacity)
 
     return jax.shard_map(device_step, mesh=mesh, in_specs=(row_spec, row_spec, row_spec, head_spec, head_spec, head_spec, out_spec, expert_spec, expert_spec, expert_spec), out_specs=row_spec, check_vma=False)

time: 345 us -> 304 us (0.88)
  Pallas kernels: 28.9 us -> 145 us
  blocking collectives: 98 us -> 40.9 us
  waiting for transfers between devices: 116 us -> 59.5 us
  matrix products: 51.7 us -> 17.5 us
  local copies, waits for them, and re-layouts: 22.3 us -> 15.8 us
  starting transfers between devices: 10.2 us -> 4.44 us
    pallas_call x0 -> x1, Pallas kernels: none -> 116 us  [run_experts(): pl.pallas_call(functools.partial(expert_body, cp, tp), out_shape=jax.Shap...]
    all_to_all x1 -> x0, blocking collectives: 57.1 us -> none  [device_step(): lax.all_to_all(send_buf.reshape(n_micro, experts, capacity, hidden), ('cp...]
    all_to_all x1 -> x0, waiting for transfers between devices: 51.5 us -> none  [device_step(): lax.all_to_all(expert_out.reshape(n_micro, experts, capacity, hidden), ('...]
    dot_general x5 -> x0, matrix products: 33.8 us -> none  [the longest x1 20.9 us: device_step(): jnp.einsum('btf,fh->bth', mixed_act, w_down[0], preferred_element_type=jn...]
    all_to_all x1 -> x0, starting transfers between devices: 5.79 us -> none  [device_step(): lax.all_to_all(expert_out.reshape(n_micro, experts, capacity, hidden), ('...]
    reshape x2 -> x0, local copies, waits for them, and re-layouts: 5.3 us -> none  [the longest x1 4.73 us: device_step(): expert_out.reshape(n_micro, experts, capacity, hidden)]
    unnamed x20 -> x15, local copies, waits for them, and re-layouts: 7.48 us -> 10.1 us
  transfers between devices with their start and end apart: 4 -> 3, of which waited for: 3 -> 2; matrix products, arithmetic and copies ran while one was open for 7% -> 9% of each run, Pallas kernels for 9% -> 10%
where the time goes in v2:
time: 304 us; the launch traced here: 299 us
  Pallas kernels  145 us (48%)
  waiting for transfers between devices  59.5 us (20%)
  blocking collectives  40.9 us (13%)
  matrix products  17.5 us (6%)
  local copies, waits for them, and re-layouts  15.8 us (5%)
  between operations  13.6 us (4%)
  starting transfers between devices  4.44 us (1%)
    pallas_call x1, Pallas kernels, run_experts(): pl.pallas_call(functools.partial(expert_body, cp, tp), out_shape=jax.Shap...  116 us
    all_gather x1, waiting for transfers between devices, device_step(): x_half = lax.all_gather(act_in, 'tp', axis=1, tiled=True)  45.2 us
    all_to_all x1, blocking collectives, device_step(): lax.all_to_all(qkv.reshape(n_micro * heads, half_rows, 3 * head_dim), 'cp...  40.9 us
    pallas_call x1, Pallas kernels, attend_unit(): pl.pallas_call(functools.partial(attention_body, pieces, piece_len, head_...  28.9 us
    all_to_all x1, waiting for transfers between devices, device_step(): lax.all_to_all(o_unit.reshape(experts, tokens, head_dim), ('cp', 'tp'), 0...  12.8 us
    dot_general x1, matrix products, device_step(): jnp.einsum('bsh,hnd->bnsd', x_half, w_qkv, preferred_element_type=jnp.flo...  10.7 us
    unnamed x15, local copies, waits for them, and re-layouts  10.1 us
    dot_general x1, matrix products, device_step(): jnp.einsum('bsk,kh->bsh', o_rows, w_full.reshape(tp_size * heads * head_d...  6.69 us
  transfers between devices with their start and end apart: 3, of which 2 were waited for; matrix products, arithmetic and copies ran while one was open for 9% of the time, Pallas kernels for 10%

profile of v2, /device:TPU:97, one launch (start us, length us, event | category | flops | bytes accessed | tf_op | source)
XLA Modules:
  0.0 299.3 jit_solution(11779287802443946956)
XLA Ops:
  6.5 0.0 copy-start
  6.5 0.0 all-gather.3.cloned.1.call-start
  6.6 0.7 all-gather.3.cloned.1.call-update
  7.3 0.1 all-gather.5.cloned.1.call-start
  7.4 0.7 all-gather.5.cloned.1.call-update
  8.1 2.4 copy.97
  10.6 2.4 copy.96
  13.0 0.0 copy-done
  13.0 2.0 copy.95
  15.0 45.2 %all-gather.3.cloned.1.call-done = bf16[2,1024,2048]{2,1,0:T(8,128)(2,1)} async-done(((bf16[2,128,2048]{2,1,0:T(8,128)(2,1)}), bf16[2,1024,2048]{2,1,0:T(8,128)(2,1)}) %all-gather.3.cloned.1.call-update) | async-done | bytes 8388624 | tf_op jit(solution)/shard_map/all_gather | solution.py:286
  60.2 10.7 %convert_bitcast_fusion = bf16[2,2,1024,384]{2,3,0,1:T(8,128)(2,1)} fusion(bf16[2,1024,2048]{2,1,0:T(8,128)(2,1)} %all-gather.3.cloned.1.call-done, bf16[2048,2,128]{0,2,1:T(8,128)(2,1)S(1)} %copy.97, bf16[2048,2,128]{0,2,1:T(8,128)(2,1)S(1)} %copy.96, bf16[2048,2,128]{0,2,1:T(8,128)(2,1)} %copy.95), kind=kOutput, calls=%fused_computation.7 | convolution fusion | flops 6453460992 | bytes 14680064 | tf_op jit(solution)/shard_map/bsh,hnd->bnsd/dot_general | solution.py:288
  70.9 3.4 %copy.98 = bf16[2,2,1024,384]{3,2,1,0:T(8,128)(2,1)S(1)} copy(bf16[2,2,1024,384]{2,3,0,1:T(8,128)(2,1)} %convert_bitcast_fusion) | data formatting | bytes 6291456 | tf_op jit(solution)/shard_map/convert_element_type | solution.py:288
  74.3 40.9 %all_to_all.10 = bf16[4,1024,384]{2,1,0:T(8,128)(2,1)S(1)} all-to-all(bf16[4,1024,384]{2,1,0:T(8,128)(2,1)S(1)} %bitcast.44), channel_id=1, replica_groups=mesh['data'=1,'cp'=4,'tp'=8] {'cp'}, dimensions={0} | all-to-all | bytes 6291456 | tf_op jit(solution)/shard_map/all_to_all | solution.py:289
  115.3 0.0 copy-start.2
  115.3 0.0 copy-start.3
  115.3 28.9 %shard_map.100 = bf16[4096,128]{1,0:T(8,128)(2,1)} custom-call(bf16[4096,384]{1,0:T(8,128)(2,1)S(1)} %bitcast.43), custom_call_target="tpu_custom_call" | custom-call | flops 4831838208 | bytes 4194304 | tf_op jit(solution)/shard_map/pallas_call | solution.py:62
  144.2 0.0 copy-start.1
  144.2 4.4 %all-to-all-start.1 = ((bf16[32,128,128]{2,1,0:T(8,128)(2,1)}), bf16[32,128,128]{2,1,0:T(8,128)(2,1)S(1)}, u32[]{:S(2)}, u32[]{:S(2)}) async-start(bf16[32,128,128]{2,1,0:T(8,128)(2,1)} %bitcast.6), calls=%async_computation.1 | async-start | bytes 2097152 | tf_op jit(solution)/shard_map/all_to_all | solution.py:291
  148.6 0.0 copy-done.2
  148.6 0.1 copy.100
  148.8 0.1 eq.55
  148.9 0.2 fusion.10
  149.1 0.1 convert_element_type.39
  149.3 0.1 copy.101
  149.3 0.1 select_add_fusion
  149.4 0.2 fusion.11
  149.6 0.8 convert_element_type.40.sel_ref
  150.4 0.0 copy-done.3
  150.4 0.8 copy.102.g_ref
  151.2 1.0 fusion.12.pick_ref
  152.2 12.8 %all-to-all-done.1 = bf16[32,128,128]{2,1,0:T(8,128)(2,1)S(1)} async-done(((bf16[32,128,128]{2,1,0:T(8,128)(2,1)}), bf16[32,128,128]{2,1,0:T(8,128)(2,1)S(1)}, u32[]{:S(2)}, u32[]{:S(2)}) %all-to-all-start.1) | async-done | bytes 1048608 | tf_op jit(solution)/shard_map/all_to_all | solution.py:291
  165.0 1.1 copy.107
  166.1 0.8 reshape.42
  166.9 0.0 all-gather.5.cloned.1.call-done
  166.9 0.0 copy-done.1
  167.0 6.7 %fusion.6.h_ref = bf16[2,128,2048]{2,1,0:T(8,128)(2,1)} fusion(bf16[2,128,2048]{2,1,0:T(8,128)(2,1)S(1)} %reshape.42, bf16[2048,2048,1]{1,0,2:T(8,128)(2,1)} %bitcast.50, bf16[2,128,2048]{2,1,0:T(8,128)(2,1)S(1)} %copy-done.1), kind=kOutput, calls=%fused_computation.9 | convolution fusion | flops 2149056512 | bytes 11534336 | tf_op jit(solution)/shard_map/bsk,kh->bsh/dot_general | solution.py:293
  173.6 116.5 %shard_map.101 = bf16[2,128,2048]{2,1,0:T(8,128)(2,1)} custom-call(bf16[2,128,2048]{2,1,0:T(8,128)(2,1)} %fusion.6.h_ref, bf16[2,512,128]{2,1,0:T(8,128)(2,1)} %convert_element_type.40.sel_ref, bf16[2,256,512]{2,1,0:T(8,128)(2,1)} %fusion.12.pick_ref, f32[2,128,2]{2,1,0:T(8,128)} %copy.102.g_ref, bf16[2048,1408]{1,0:T(8,128)(2,1)} %bitcast.51, ...), custom_call_target="tpu_custom_call" | custom-call | flops 17716740096 | bytes 17301504 | tf_op jit(solution)/shard_map/pallas_call | solution.py:258
  290.1 2.3 copy.110
  (3 shorter events, 0.0 us)
Async XLA Ops:
  6.5 6.5 %copy-start = (bf16[2048,2,128]{2,1,0:T(2,128)(2,1)S(1)}, bf16[2048,2,128]{2,1,0:T(2,128)(2,1)}, u32[]{:S(2)}) copy-start(bf16[2048,2,128]{2,1,0:T(2,128)(2,1)} %param.13) | copy-start | bytes 3145732
  6.5 53.7 %all-gather.3.cloned.1.call-start = ((), (), s32[]{:S(2)}) async-start(), calls=%async_computation.2 | async-start | bytes 9437184 | tf_op jit(solution)/shard_map/all_gather | solution.py:286
  7.3 159.6 %all-gather.5.cloned.1.call-start = ((), (), s32[]{:S(2)}) async-start(), calls=%async_computation.3 | async-start | bytes 9437184 | tf_op jit(solution)/shard_map/all_gather | solution.py:287
  115.3 33.3 %copy-start.2 = (s32[2,128,2]{1,2,0:T(2,128)S(1)}, s32[2,128,2]{1,2,0:T(2,128)}, u32[]{:S(2)}) copy-start(s32[2,128,2]{1,2,0:T(2,128)} %param.11) | copy-start | bytes 6148
  115.3 35.1 %copy-start.3 = (f32[2,128,2]{1,2,0:T(2,128)S(1)}, f32[2,128,2]{1,2,0:T(2,128)}, u32[]{:S(2)}) copy-start(f32[2,128,2]{1,2,0:T(2,128)} %param.12) | copy-start | bytes 6148
  144.2 22.7 %copy-start.1 = (bf16[2,128,2048]{2,1,0:T(8,128)(2,1)S(1)}, bf16[2,128,2048]{2,1,0:T(8,128)(2,1)}, u32[]{:S(2)}) copy-start(bf16[2,128,2048]{2,1,0:T(8,128)(2,1)} %param.10) | copy-start | bytes 3145732
  144.2 20.8 %all-to-all-start.1 = ((bf16[32,128,128]{2,1,0:T(8,128)(2,1)}), bf16[32,128,128]{2,1,0:T(8,128)(2,1)S(1)}, u32[]{:S(2)}, u32[]{:S(2)}) async-start(bf16[32,128,128]{2,1,0:T(8,128)(2,1)} %bitcast.6), calls=%async_computation.1 | async-start | bytes 2097152 | tf_op jit(solution)/shard_map/all_to_all | solution.py:291
Sparse Core Ops, SparseCore 0:
  8.9 51.2 all-gather.2
  61.9 47.1 all-gather.4

commit v3 on v2

--- a/solution.py
+++ b/solution.py
@@ -10,19 +10,143 @@
 LOG2E = 1.4426950408889634
 
 
-def attention_body(pieces, piece_len, head_dim, qkv_ref, o_ref, s_ref):
-    p = pl.program_id(0)
-    half = pieces // 2
+MESH_ID = pl.DeviceIdType.MESH
+
+
+def front_body(cp, tp, heads, x_hbm, w_hbm, wo_hbm, h_ref, xg, wo, w, u, q_out, s_ref, o_st, o_rows,
+               in_sem, x_sem, wo_sem, u_sem, o_sem):
+    d, c, t = lax.axis_index('data'), lax.axis_index('cp'), lax.axis_index('tp')
+    nx = tp // 2
+    x, k = t // 2, t % 2
+    tokens, hidden = x_hbm.shape[1], x_hbm.shape[2]
+    half_rows = tokens * tp
+    pieces = 2 * cp
+    piece_len = half_rows // 2
+    head_dim = o_st.shape[1]
+    width = 3 * head_dim
+    left, right, far = ((x + nx - 1) % nx) * 2, ((x + 1) % nx) * 2, ((x + 2) % nx) * 2
+    mine, other = k, 1 - k
+    mate = 2 * x + other
+
+    loads = [pltpu.make_async_copy(x_hbm, xg.at[t], in_sem.at[0]), pltpu.make_async_copy(w_hbm, w, in_sem.at[1]), pltpu.make_async_copy(wo_hbm, wo.at[t], in_sem.at[2])]
+    for load in loads:
+        load.start()
+    barrier = pltpu.get_barrier_semaphore()
+    peers = [(dc, dt) for dc in range(cp) for dt in range(tp) if dc or dt]
+    for dc, dt in peers:
+        pl.semaphore_signal(barrier, inc=1, device_id=(d, (c + dc) % cp, (t + dt) % tp), device_id_type=MESH_ID)
+    pl.semaphore_wait(barrier, len(peers))
+
+    def send(src, dst, sems, key, cc, tt):
+        return pltpu.make_async_remote_copy(src_ref=src, dst_ref=dst, send_sem=sems.at[(0,) + key], recv_sem=sems.at[(1,) + key], device_id=(d, cc, tt), device_id_type=MESH_ID)
+
+    names = ['r0', 'r1', 'r2', 'l0', 'l1', 'l2'] + ['p%d' % i for i in range(8)]
+
+    def ring(buf, sems):
+        sent = {}
+
+        def start(name, src, part, target):
+            sent[name] = send(buf.at[src, part], buf.at[src, part], sems, (names.index(name),), c, target)
+            sent[name].start()
+
+        def wave(n):
+            if n == 0:
+                start('p0', t, 0, mate)
+                start('p1', t, 1, mate)
+                start('r0', t, 0, right + mine)
+                start('l0', t, 1, left + mine)
+                start('r1', t, 1, right + mine)
+                start('l1', t, 0, left + mine)
+            elif n == 1:
+                sent['r0'].wait_recv()
+                start('r2', left + mine, 0, right + mine)
+                start('p2', left + mine, 0, mate)
+                sent['l0'].wait_recv()
+                start('l2', right + mine, 1, left + mine)
+                start('p3', right + mine, 1, mate)
+            elif n == 2:
+                sent['r1'].wait_recv()
+                start('p4', left + mine, 1, mate)
+                sent['l1'].wait_recv()
+                start('p5', right + mine, 0, mate)
+            else:
+                sent['r2'].wait_recv()
+                start('p6', far + mine, 0, mate)
+                sent['l2'].wait_recv()
+                start('p7', far + mine, 1, mate)
+        return sent, wave
+
+    x_sent, x_wave = ring(xg, x_sem)
+    wo_sent, wo_wave = ring(wo, wo_sem)
+    u_sent = {}
+
+    def project(tt, s):
+        @pl.loop(0, heads * width // 256)
+        def _(n):
+            at = pl.ds(pl.multiple_of(n * 256, 256), 256)
+            q_out[tt, s, :, at] = jnp.dot(xg[tt, s], w[:, at], preferred_element_type=jnp.float32).astype(jnp.bfloat16)
+
+        rows = pl.ds(pl.multiple_of(c * half_rows + tt * tokens, tokens), tokens)
+        for dc in (1, cp - 1, 2):
+            c2 = (c + dc) % cp
+            lanes = pl.ds(pl.multiple_of(c2 % heads * width, 128), width)
+            copy = send(q_out.at[tt, s, :, lanes], u.at[rows], u_sem, (dc, tt), c2, t)
+            pl.when(c2 // heads == s)(copy.start)
+            u_sent.setdefault(dc, []).append(copy)
+
+        @pl.when(c // heads == s)
+        def _():
+            lanes = pl.ds(pl.multiple_of(c % heads * width, 128), width)
+            u[rows] = q_out[tt, s, :, lanes]
+
+    loads[0].wait()
+    x_wave(0)
+    loads[1].wait()
+    project(t, 0)
+    project(t, 1)
+    for s, name in ((0, 'p0'), (1, 'p1')):
+        x_sent[name].wait_recv()
+        project(mate, s)
+    x_wave(1)
+    loads[2].wait()
+    wo_wave(0)
+    project(left + mine, 0)
+    project(right + mine, 1)
+    x_sent['p2'].wait_recv()
+    project(left + other, 0)
+    x_sent['p3'].wait_recv()
+    project(right + other, 1)
+    x_wave(2)
+    project(left + mine, 1)
+    project(right + mine, 0)
+    x_sent['p4'].wait_recv()
+    project(left + other, 1)
+    x_sent['p5'].wait_recv()
+    project(right + other, 0)
+    x_wave(3)
+    project(far + mine, 0)
+    project(far + mine, 1)
+    x_sent['p6'].wait_recv()
+    project(far + other, 0)
+    x_sent['p7'].wait_recv()
+    project(far + other, 1)
+
+    def u_copy(dc, tt):
+        c2 = (c + dc) % cp
+        lanes = pl.ds(pl.multiple_of(c2 % heads * width, 128), width)
+        rows = pl.ds(pl.multiple_of(c * half_rows + tt * tokens, tokens), tokens)
+        return send(q_out.at[tt, c2 // heads, :, lanes], u.at[rows], u_sem, (dc, tt), c2, t)
+
+    for dc in (1, cp - 1, 2):
+        for tt in range(tp):
+            u_copy(dc, tt).wait_recv()
+    wo_wave(1)
+
     factor = head_dim ** -0.5 * LOG2E
+    per_half = tp // 2
 
     def offset(n):
-        return pl.multiple_of(jnp.where(n < half, 2 * piece_len * n, 2 * piece_len * (pieces - 1 - n) + piece_len), piece_len)
-
-    q_rows = qkv_ref[pl.ds(offset(p), piece_len), 0:head_dim]
-
-    def scores(n):
-        k_rows = qkv_ref[pl.ds(offset(n), piece_len), head_dim:2 * head_dim]
-        return lax.dot_general(q_rows, k_rows, (((1,), (1,)), ((), ())), preferred_element_type=jnp.float32)
+        return pl.multiple_of(jnp.where(n < cp, 2 * piece_len * n, 2 * piece_len * (pieces - 1 - n) + piece_len), piece_len)
 
     def fold(op, wide):
         parts = [wide[:, i * 128:(i + 1) * 128] for i in range(piece_len // 128)]
@@ -30,48 +154,101 @@
             parts = [op(a, b) for a, b in zip(parts[::2], parts[1::2])]
         return parts[0]
 
-    def first(n, peak):
-        s = scores(n)
-        s_ref[n] = s
-        return jnp.maximum(peak, fold(jnp.maximum, s))
-
     row = lax.broadcasted_iota(jnp.int32, (piece_len, piece_len), 0)
     col = lax.broadcasted_iota(jnp.int32, (piece_len, piece_len), 1)
-    s_diag = jnp.where(col <= row, scores(p), -jnp.inf)
-    s_ref[p] = s_diag
-    peak = lax.fori_loop(0, p, first, fold(jnp.maximum, s_diag))
-    peak = jnp.max(peak, axis=1, keepdims=True) * factor
-
-    def second(n, carry):
-        total, acc = carry
-        e = jnp.exp2(s_ref[n] * factor - peak)
-        v_rows = qkv_ref[pl.ds(offset(n), piece_len), 2 * head_dim:3 * head_dim]
-        acc = acc + jnp.dot(e.astype(jnp.bfloat16), v_rows, preferred_element_type=jnp.float32)
-        return total + fold(jnp.add, e), acc
-
-    zero = jnp.zeros((piece_len, 128), jnp.float32)
-    total, acc = lax.fori_loop(0, p + 1, second, (zero, jnp.zeros((piece_len, head_dim), jnp.float32)))
-    total = jnp.sum(total, axis=1, keepdims=True)
-    o_ref[pl.ds(offset(p), piece_len), :] = (acc / total).astype(jnp.bfloat16)
-
-
-def attend_unit(qkv, pieces):
-    rows, width = qkv.shape
-    head_dim = width // 3
-    piece_len = rows // pieces
+    unit_seq = c // heads
+    unit_head = t * heads + c % heads
+
+    def o_copy(rows, dcl, dtl, cc, tt):
+        lanes = pl.ds(pl.multiple_of(unit_head * head_dim, 128), head_dim)
+        return send(o_st.at[rows], o_rows.at[unit_seq, :, lanes], o_sem, (dcl, dtl), cc, tt)
+
+    @pl.loop(0, pieces)
+    def _(p):
+        q_rows = u[pl.ds(offset(p), piece_len), 0:head_dim]
+
+        def scores(n):
+            k_rows = u[pl.ds(offset(n), piece_len), head_dim:2 * head_dim]
+            return lax.dot_general(q_rows, k_rows, (((1,), (1,)), ((), ())), preferred_element_type=jnp.float32)
+
+        def first(n, peak):
+            s = scores(n)
+            s_ref[n] = s
+            return jnp.maximum(peak, fold(jnp.maximum, s))
+
+        s_diag = jnp.where(col <= row, scores(p), -jnp.inf)
+        s_ref[p] = s_diag
+        peak = lax.fori_loop(0, p, first, fold(jnp.maximum, s_diag))
+        peak = jnp.max(peak, axis=1, keepdims=True) * factor
+
+        def second(n, carry):
+            total, acc = carry
+            e = jnp.exp2(s_ref[n] * factor - peak)
+            v_rows = u[pl.ds(offset(n), piece_len), 2 * head_dim:3 * head_dim]
+            acc = acc + jnp.dot(e.astype(jnp.bfloat16), v_rows, preferred_element_type=jnp.float32)
+            return total + fold(jnp.add, e), acc
+
+        total, acc = lax.fori_loop(0, p + 1, second, (jnp.zeros((piece_len, 128), jnp.float32), jnp.zeros((piece_len, head_dim), jnp.float32)))
+        total = jnp.sum(total, axis=1, keepdims=True)
+        o_st[pl.ds(offset(p), piece_len), :] = (acc / total).astype(jnp.bfloat16)
+        low = p < cp
+        cc = jnp.where(low, p, pieces - 1 - p)
+        for i in range(per_half):
+            tt = jnp.where(low, i, per_half + i)
+            rows = pl.ds(pl.multiple_of(offset(p) + i * tokens, tokens), tokens)
+            dcl, dtl = (cc - c + cp) % cp, (tt - t + tp) % tp
+            pl.when(dcl + dtl > 0)(o_copy(rows, dcl, dtl, cc, tt).start)
+
+            @pl.when(dcl + dtl == 0)
+            def _():
+                lanes = pl.ds(pl.multiple_of(unit_head * head_dim, 128), head_dim)
+                o_rows[unit_seq, :, lanes] = o_st[rows]
+
+    wo_wave(2)
+    wo_wave(3)
+    for i in range(8):
+        wo_sent['p%d' % i].wait_recv()
+    first_rows = pl.ds(0, tokens)
+    o_all = [o_copy(first_rows, dc, dt, (c + dc) % cp, (t + dt) % tp) for dc, dt in peers]
+    for copy in o_all:
+        copy.wait_recv()
+
+    full = tp * heads * head_dim
+
+    @pl.loop(0, hidden // 256)
+    def _(n):
+        at = pl.ds(pl.multiple_of(n * 256, 256), 256)
+        a = jnp.dot(o_rows[...].reshape(2 * tokens, full), wo[:, :, :, at].reshape(full, 256), preferred_element_type=jnp.float32)
+        h_ref[:, :, at] = (xg[t, :, :, at].astype(jnp.float32) + a.reshape(2, tokens, 256)).astype(jnp.bfloat16)
+
+    for copy in list(x_sent.values()) + list(wo_sent.values()) + o_all:
+        copy.wait_send()
+    for dc in (1, cp - 1, 2):
+        for tt in range(tp):
+            u_copy(dc, tt).wait_send()
+
+
+def run_front(act_in, w_qkv, w_out, cp, tp, heads):
+    n_micro, tokens, hidden = act_in.shape
+    head_dim = w_out.shape[1]
+    half_rows = tokens * tp
+    rows = cp * half_rows
+    bf16 = jnp.bfloat16
+    any_spec = pl.BlockSpec(memory_space=pl.ANY)
+    dma = pltpu.SemaphoreType.DMA
+    vmem = [(tp, n_micro, tokens, hidden), (tp, heads, head_dim, hidden), (hidden, heads * 3 * head_dim), (rows, 3 * head_dim), (tp, n_micro, tokens, heads * 3 * head_dim)]
+    piece = half_rows // 2
     return pl.pallas_call(
-        functools.partial(attention_body, pieces, piece_len, head_dim),
-        grid=(pieces,),
-        out_shape=jax.ShapeDtypeStruct((rows, head_dim), jnp.bfloat16),
-        in_specs=[pl.BlockSpec((rows, width), lambda p: (0, 0))],
-        out_specs=pl.BlockSpec((rows, head_dim), lambda p: (0, 0)),
-        scratch_shapes=[pltpu.VMEM((pieces, piece_len, piece_len), jnp.float32)],
-        compiler_params=pltpu.CompilerParams(vmem_limit_bytes=40 << 20),
-        cost_estimate=pl.CostEstimate(flops=9 * 4 * rows * rows * head_dim // 16, bytes_accessed=4 * rows * head_dim * 2, transcendentals=0),
-    )(qkv)
-
-
-MESH_ID = pl.DeviceIdType.MESH
+        functools.partial(front_body, cp, tp, heads),
+        out_shape=jax.ShapeDtypeStruct(act_in.shape, bf16),
+        in_specs=[any_spec] * 3,
+        out_specs=pl.BlockSpec(memory_space=pltpu.VMEM),
+        scratch_shapes=[pltpu.VMEM(s, bf16) for s in vmem]
+        + [pltpu.VMEM((2 * cp, piece, piece), jnp.float32), pltpu.VMEM((rows, head_dim), bf16), pltpu.VMEM((n_micro, tokens, tp * heads * head_dim), bf16)]
+        + [dma((3,)), dma((2, 14)), dma((2, 14)), dma((2, cp, tp)), dma((2, cp, tp))],
+        compiler_params=pltpu.CompilerParams(collective_id=2, has_side_effects=True, vmem_limit_bytes=56 << 20),
+        cost_estimate=pl.CostEstimate(flops=8 * rows * hidden * head_dim * 3, bytes_accessed=20 << 20, transcendentals=0),
+    )(act_in, w_qkv, w_out)
 
 
 def expert_body(cp, tp, h_ref, sel_ref, pick_ref, g_ref, wg_hbm, wu_hbm, wd_hbm, y_ref,
@@ -281,17 +458,8 @@
     def device_step(act_in, route_ids, route_gates, w_query, w_key, w_value, w_out, w_gate, w_up, w_down):
         n_micro, tokens, hidden = act_in.shape
         heads, head_dim = w_query.shape[1], w_query.shape[2]
-        half_rows = tokens * tp_size
-        w_qkv = jnp.concatenate([w_query, w_key, w_value], axis=2)
-        x_half = lax.all_gather(act_in, 'tp', axis=1, tiled=True)
-        w_full = lax.all_gather(w_out, 'tp', axis=0, tiled=True)
-        qkv = jnp.einsum('bsh,hnd->bnsd', x_half, w_qkv, preferred_element_type=jnp.float32).astype(jnp.bfloat16)
-        unit = lax.all_to_all(qkv.reshape(n_micro * heads, half_rows, 3 * head_dim), 'cp', 0, 0, tiled=True)
-        o_unit = attend_unit(unit.reshape(cp_size * half_rows, 3 * head_dim), 2 * cp_size)
-        o_recv = lax.all_to_all(o_unit.reshape(experts, tokens, head_dim), ('cp', 'tp'), 0, 0, tiled=True)
-        o_rows = o_recv.reshape(n_micro, heads, tp_size, tokens, head_dim).transpose(0, 3, 2, 1, 4).reshape(n_micro, tokens, tp_size * heads * head_dim)
-        attn = jnp.einsum('bsk,kh->bsh', o_rows, w_full.reshape(tp_size * heads * head_dim, hidden), preferred_element_type=jnp.float32)
-        mid_rows = (act_in.astype(jnp.float32) + attn).astype(jnp.bfloat16)
+        w_qkv = jnp.concatenate([w_query, w_key, w_value], axis=2).reshape(hidden, heads * 3 * head_dim)
+        mid_rows = run_front(act_in, w_qkv, w_out, cp_size, tp_size, heads)
 
         capacity = (4 * tokens) // experts
         slots = experts * capacity

time: 304 us -> 230 us (0.76); the launches traced: 299 us -> 230 us
  Pallas kernels: 145 us -> 216 us
  waiting for transfers between devices: 59.5 us -> 0 us
  blocking collectives: 40.9 us -> 0 us
  matrix products: 17.5 us -> 0.21 us
  between operations: 13.6 us -> 0.08 us
  local copies, waits for them, and re-layouts: 15.8 us -> 5.9 us
  other arithmetic: 2.03 us -> 7.8 us
  starting transfers between devices: 4.44 us -> 0 us
    pallas_call x1, Pallas kernels: 28.9 us -> 95.7 us  [run_front(): pl.pallas_call(functools.partial(front_body, cp, tp, heads), out_shape=ja...]
    all_gather x2 -> x0, waiting for transfers between devices: 45.2 us -> none  [the longest x1 45.2 us: device_step(): x_half = lax.all_gather(act_in, 'tp', axis=1, tiled=True)]
    all_to_all x1 -> x0, blocking collectives: 40.9 us -> none  [device_step(): lax.all_to_all(qkv.reshape(n_micro * heads, half_rows, 3 * head_dim), 'cp...]
    dot_general x2 -> x0, matrix products: 17.3 us -> none  [the longest x1 10.7 us: device_step(): jnp.einsum('bsh,hnd->bnsd', x_half, w_qkv, preferred_element_type=jnp.flo...]
    all_to_all x1 -> x0, waiting for transfers between devices: 12.8 us -> none  [device_step(): lax.all_to_all(o_unit.reshape(experts, tokens, head_dim), ('cp', 'tp'), 0...]
    concatenate x0 -> x1, other arithmetic: none -> 5.82 us  [device_step(): jnp.concatenate([w_query, w_key, w_value], axis=2)]
    unnamed x15 -> x9, local copies, waits for them, and re-layouts: 10.1 us -> 5.54 us
    all_to_all x1 -> x0, starting transfers between devices: 4.38 us -> none  [device_step(): lax.all_to_all(o_unit.reshape(experts, tokens, head_dim), ('cp', 'tp'), 0...]
  transfers between devices with their start and end apart: 3 -> 0, of which waited for: 2 -> 0; matrix products, arithmetic and copies ran while one was open for 9% -> 0% of each run, Pallas kernels for 10% -> 0%
where the time goes in v3:
time: 230 us
  Pallas kernels  216 us (94%)
  other arithmetic  7.8 us (3%)
  local copies, waits for them, and re-layouts  5.9 us (3%)
    pallas_call x1, Pallas kernels, run_experts(): pl.pallas_call(functools.partial(expert_body, cp, tp), out_shape=jax.Shap...  120 us
    pallas_call x1, Pallas kernels, run_front(): pl.pallas_call(functools.partial(front_body, cp, tp, heads), out_shape=ja...  95.7 us
    concatenate x1, other arithmetic, device_step(): jnp.concatenate([w_query, w_key, w_value], axis=2)  5.82 us
    unnamed x9, local copies, waits for them, and re-layouts  5.54 us

profile of v3, /device:TPU:97, one launch (start us, length us, event | category | flops | bytes accessed | tf_op | source)
XLA Modules:
  0.0 229.9 jit_solution(6296125365444014279)
XLA Ops:
  0.0 5.8 %pad_maximum_fusion = bf16[2048,2,384]{2,1,0:T(2,128)(2,1)S(1)} fusion(bf16[2048,2,128]{2,1,0:T(2,128)(2,1)} %param.15, bf16[2048,2,128]{2,1,0:T(2,128)(2,1)} %param.14, bf16[2048,2,128]{2,1,0:T(2,128)(2,1)} %param.13), kind=kLoop, calls=%fused_computation | loop fusion | flops 9437184 | bytes 6291456 | tf_op jit(solution)/shard_map/concatenate | solution.py:461
  5.8 2.3 %copy.59 = bf16[256,8,2,384]{3,1,2,0:T(8,128)(2,1)} copy(bf16[256,8,2,384]{3,2,1,0:T(2,128)(2,1)S(1)} %bitcast.19) | data formatting | bytes 6291456
  8.1 0.0 copy-start
  8.1 0.0 copy-start.1
  8.1 95.7 %shard_map.100.h_ref = bf16[2,128,2048]{2,1,0:T(8,128)(2,1)} custom-call(bf16[2,128,2048]{2,1,0:T(8,128)(2,1)} %x_hbm.1, bf16[2048,768]{1,0:T(8,128)(2,1)} %bitcast.20, bf16[2,128,2048]{2,1,0:T(8,128)(2,1)} %wo_hbm.1), custom_call_target="tpu_custom_call" | custom-call | flops 25769803776 | bytes 20971520 | tf_op jit(solution)/shard_map/pallas_call | solution.py:241
  103.9 0.0 copy-done
  103.9 0.1 copy.56
  104.0 0.1 eq.55
  104.2 0.2 fusion.1
  104.4 0.1 convert_element_type.23
  104.5 0.1 copy.57
  104.6 0.1 select_add_fusion
  104.7 0.2 fusion.2
  104.9 0.8 convert_element_type.24.sel_ref
  105.7 0.9 fusion.3.pick_ref
  106.6 0.0 copy-done.1
  106.6 0.8 copy.58.g_ref
  107.4 120.2 %shard_map.101 = bf16[2,128,2048]{2,1,0:T(8,128)(2,1)} custom-call(bf16[2,128,2048]{2,1,0:T(8,128)(2,1)} %shard_map.100.h_ref, bf16[2,512,128]{2,1,0:T(8,128)(2,1)} %convert_element_type.24.sel_ref, bf16[2,256,512]{2,1,0:T(8,128)(2,1)} %fusion.3.pick_ref, f32[2,128,2]{2,1,0:T(8,128)} %copy.58.g_ref, bf16[2048,1408]{1,0:T(8,128)(2,1)} %bitcast.24, ...), custom_call_target="tpu_custom_call" | custom-call | flops 17716740096 | bytes 17301504 | tf_op jit(solution)/shard_map/pallas_call | solution.py:435
  227.6 2.3 %copy.64 = bf16[2,128,2048]{2,1,0:T(8,128)(2,1)} copy(bf16[2,128,2048]{2,1,0:T(8,128)(2,1)} %shard_map.101) | data formatting | bytes 2097152
  (3 shorter events, 0.0 us)
Async XLA Ops:
  8.1 95.7 %copy-start = (s32[2,128,2]{1,2,0:T(2,128)S(1)}, s32[2,128,2]{1,2,0:T(2,128)}, u32[]{:S(2)}) copy-start(s32[2,128,2]{1,2,0:T(2,128)} %param.11) | copy-start | bytes 6148
  8.1 98.5 %copy-start.1 = (f32[2,128,2]{1,2,0:T(2,128)S(1)}, f32[2,128,2]{1,2,0:T(2,128)}, u32[]{:S(2)}) copy-start(f32[2,128,2]{1,2,0:T(2,128)} %param.12) | copy-start | bytes 6148

commit v4 on v3

v4 whole, which is shorter than its diff:
```python
import functools

import jax
import jax.numpy as jnp
from jax import lax
from jax.experimental import pallas as pl
from jax.experimental.pallas import tpu as pltpu
from jax.sharding import PartitionSpec as P

LOG2E = 1.4426950408889634


MESH_ID = pl.DeviceIdType.MESH


def front_body(cp, tp, heads, x_hbm, wq_hbm, wk_hbm, wv_hbm, wo_hbm, h_ref, xg, wo, w, u, q_out, s_ref, o_st, o_rows,
               peaks, totals, accs, raw, in_sem, x_sem, bulk_sem, strip_sem, lane_sem, mate_sem, u_sem, o_sem):
    d, c, t = lax.axis_index('data'), lax.axis_index('cp'), lax.axis_index('tp')
    nx = tp // 2
    x, k = t // 2, t % 2
    tokens, hidden = x_hbm.shape[1], x_hbm.shape[2]
    half_rows = tokens * tp
    pieces = 2 * cp
    piece_len = half_rows // 2
    head_dim = o_st.shape[1]
    width = 3 * head_dim
    left, right, far = ((x + nx - 1) % nx) * 2, ((x + 1) % nx) * 2, ((x + 2) % nx) * 2
    mine, other = k, 1 - k
    mate = 2 * x + other

    split = wo_hbm.shape[0] - 16 * cp
    strip_rows = pl.ds(split + 16 * c, 16)
    loads = [pltpu.make_async_copy(x_hbm, xg.at[t], in_sem.at[0]), pltpu.make_async_copy(wq_hbm, raw.at[0], in_sem.at[1]), pltpu.make_async_copy(wo_hbm.at[pl.ds(0, split)], wo.at[x, k, pl.ds(0, split)], in_sem.at[2]),
             pltpu.make_async_copy(wo_hbm.at[strip_rows], wo.at[x, k, strip_rows], in_sem.at[3]),
             pltpu.make_async_copy(wk_hbm, raw.at[1], in_sem.at[4]), pltpu.make_async_copy(wv_hbm, raw.at[2], in_sem.at[5])]
    for load in loads:
        load.start()
    barrier = pltpu.get_barrier_semaphore()
    peers = [(dc, dt) for dc in range(cp) for dt in range(tp) if dc or dt]
    for dc, dt in peers:
        pl.semaphore_signal(barrier, inc=1, device_id=(d, (c + dc) % cp, (t + dt) % tp), device_id_type=MESH_ID)
    pl.semaphore_wait(barrier, len(peers))

    def send(src, dst, sems, key, cc, tt):
        return pltpu.make_async_remote_copy(src_ref=src, dst_ref=dst, send_sem=sems.at[(0,) + key], recv_sem=sems.at[(1,) + key], device_id=(d, cc, tt), device_id_type=MESH_ID)

    names = ['r0', 'r1', 'r2', 'l0', 'l1', 'l2'] + ['p%d' % i for i in range(8)]

    def ring(view, sems, with_mate):
        sent = {}

        def start(name, src, part, target):
            if with_mate or name[0] != 'p':
                sent[name] = send(view(src, part), view(src, part), sems, (names.index(name),), c, target)
                sent[name].start()

        def wave(n):
            if n == 0:
                start('p0', t, 0, mate)
                start('p1', t, 1, mate)
                start('r0', t, 0, right + mine)
                start('l0', t, 1, left + mine)
                start('r1', t, 1, right + mine)
                start('l1', t, 0, left + mine)
            elif n == 1:
                sent['r0'].wait_recv()
                start('r2', left + mine, 0, right + mine)
                start('p2', left + mine, 0, mate)
                sent['l0'].wait_recv()
                start('l2', right + mine, 1, left + mine)
                start('p3', right + mine, 1, mate)
            elif n == 2:
                sent['r1'].wait_recv()
                start('p4', left + mine, 1, mate)
                sent['l1'].wait_recv()
                start('p5', right + mine, 0, mate)
            else:
                sent['r2'].wait_recv()
                start('p6', far + mine, 0, mate)
                sent['l2'].wait_recv()
                start('p7', far + mine, 1, mate)
        return sent, wave

    part_rows = split // 2

    def bulk(src, part):
        return wo.at[src // 2, src % 2, pl.ds(part * part_rows, part_rows)]

    def strip(src, part):
        return wo.at[src // 2, src % 2, pl.ds(split + 16 * c, 16), pl.ds(part * (hidden // 2), hidden // 2)]

    def lane(q):
        return wo.at[:, k, pl.ds(split + 16 * q, 16)]

    x_sent, x_wave = ring(lambda src, part: xg.at[src, part], x_sem, True)
    bulk_sent, bulk_wave = ring(bulk, bulk_sem, True)
    strip_sent, strip_wave = ring(strip, strip_sem, False)
    lane_y = {dc: send(lane(c), lane(c), lane_sem, (dc,), (c + dc) % cp, t) for dc in (1, cp - 1, 2)}
    lane_mate = {dc: send(lane((c + cp - dc) % cp), lane((c + cp - dc) % cp), mate_sem, (dc,), c, mate) for dc in (0, 1, cp - 1, 2)}

    def project(tt, s):
        @pl.loop(0, heads * width // 256)
        def _(n):
            at = pl.ds(pl.multiple_of(n * 256, 256), 256)
            q_out[tt, s, :, at] = jnp.dot(xg[tt, s], w[:, at], preferred_element_type=jnp.float32).astype(jnp.bfloat16)

        rows = pl.ds(pl.multiple_of(c * half_rows + tt * tokens, tokens), tokens)
        for dc in (1, cp - 1, 2):
            c2 = (c + dc) % cp
            lanes = pl.ds(pl.multiple_of(c2 % heads * width, 128), width)
            copy = send(q_out.at[tt, s, :, lanes], u.at[rows], u_sem, (dc, tt), c2, t)
            pl.when(c2 // heads == s)(copy.start)

        @pl.when(c // heads == s)
        def _():
            lanes = pl.ds(pl.multiple_of(c % heads * width, 128), width)
            u[rows] = q_out[tt, s, :, lanes]

    loads[0].wait()
    x_wave(0)
    loads[3].wait()
    strip_wave(0)
    for i in (1, 4, 5):
        loads[i].wait()

    @pl.loop(0, hidden // 32)
    def _(i):
        at = pl.ds(pl.multiple_of(i * 32, 32), 32)
        for j in range(3):
            flat = raw[j, at].reshape(32, heads * head_dim)
            for n in range(heads):
                w[at, n * width + j * head_dim:n * width + (j + 1) * head_dim] = flat[:, n * head_dim:(n + 1) * head_dim]

    project(t, 0)
    project(t, 1)
    for s, name in ((0, 'p0'), (1, 'p1')):
        x_sent[name].wait_recv()
        project(mate, s)
    x_wave(1)
    project(left + mine, 0)
    project(right + mine, 1)
    x_sent['p2'].wait_recv()
    project(left + other, 0)
    x_sent['p3'].wait_recv()
    project(right + other, 1)
    x_wave(2)
    strip_wave(1)
    loads[2].wait()
    bulk_wave(0)
    project(left + mine, 1)
    project(right + mine, 0)
    x_sent['p4'].wait_recv()
    project(left + other, 1)
    x_sent['p5'].wait_recv()
    project(right + other, 0)
    x_wave(3)
    project(far + mine, 0)
    project(far + mine, 1)
    x_sent['p6'].wait_recv()
    project(far + other, 0)
    x_sent['p7'].wait_recv()
    project(far + other, 1)
    strip_wave(2)
    strip_wave(3)
    for dc in (1, cp - 1, 2):
        lane_y[dc].start()
    lane_mate[0].start()

    def u_copy(dc, tt):
        c2 = (c + dc) % cp
        lanes = pl.ds(pl.multiple_of(c2 % heads * width, 128), width)
        rows = pl.ds(pl.multiple_of(c * half_rows + tt * tokens, tokens), tokens)
        return send(q_out.at[tt, c2 // heads, :, lanes], u.at[rows], u_sem, (dc, tt), c2, t)

    for dc in (1, cp - 1, 2):
        for tt in range(tp):
            u_copy(dc, tt).wait_recv()
    bulk_wave(1)

    factor = head_dim ** -0.5 * LOG2E
    per_half = tp // 2

    def offset(n):
        return pl.multiple_of(jnp.where(n < cp, 2 * piece_len * n, 2 * piece_len * (pieces - 1 - n) + piece_len), piece_len)

    def fold(op, wide):
        parts = [wide[:, i * 128:(i + 1) * 128] for i in range(piece_len // 128)]
        while len(parts) > 1:
            parts = [op(a, b) for a, b in zip(parts[::2], parts[1::2])]
        return parts[0]

    row = lax.broadcasted_iota(jnp.int32, (piece_len, piece_len), 0)
    col = lax.broadcasted_iota(jnp.int32, (piece_len, piece_len), 1)
    unit_seq = c // heads
    unit_head = t * heads + c % heads

    def o_copy(rows, dcl, dtl, cc, tt):
        lanes = pl.ds(pl.multiple_of(unit_head * head_dim, 128), head_dim)
        return send(o_st.at[rows], o_rows.at[unit_seq, :, lanes], o_sem, (dcl, dtl), cc, tt)

    gap = col - row

    @pl.loop(0, cp)
    def _(p):
        lo, hi = p, pieces - 1 - p

        def place(j):
            if j >= cp:
                return hi, j - p - 1, 1
            is_lo = j <= p
            return jnp.where(is_lo, lo, hi), jnp.where(is_lo, j, j - p - 1), jnp.where(is_lo, 0, 1)

        def scores(j):
            piece, n, _ = place(j)
            q_rows = u[pl.ds(offset(piece), piece_len), 0:head_dim]
            k_rows = u[pl.ds(offset(n), piece_len), head_dim:2 * head_dim]
            s = lax.dot_general(q_rows, k_rows, (((1,), (1,)), ((), ())), preferred_element_type=jnp.float32)
            if j == pieces:
                s = jnp.where(gap <= 0, s, -jnp.inf)
            elif j < cp:
                s = jnp.where(gap <= jnp.where(j == p, 0, piece_len), s, -jnp.inf)
            s_ref[j] = s
            return fold(jnp.maximum, s)

        high = scores(cp)
        for j in range(cp + 1, pieces + 1):
            high = jnp.maximum(high, scores(j))
        peaks[1] = high
        peaks[0] = jnp.full_like(high, -jnp.inf)
        for j in range(cp):
            slot = place(j)[2]
            peaks[slot] = jnp.maximum(peaks[slot], scores(j))
        for slot in range(2):
            peaks[slot] = jnp.broadcast_to(jnp.max(peaks[slot], axis=1, keepdims=True) * factor, high.shape)

        def weigh(j):
            _, n, slot = place(j)
            peak = peaks[slot]
            s = s_ref[j]
            e = jnp.concatenate([jnp.exp2(s[:, i * 128:(i + 1) * 128] * factor - peak) for i in range(piece_len // 128)], axis=1)
            v_rows = u[pl.ds(offset(n), piece_len), 2 * head_dim:3 * head_dim]
            return fold(jnp.add, e), jnp.dot(e.astype(jnp.bfloat16), v_rows, preferred_element_type=jnp.float32)

        total, acc = weigh(cp)
        for j in range(cp + 1, pieces + 1):
            more, part = weigh(j)
            total, acc = total + more, acc + part
        totals[0], accs[0] = jnp.zeros_like(total), jnp.zeros_like(acc)
        totals[1], accs[1] = total, acc
        for j in range(cp):
            slot = place(j)[2]
            more, part = weigh(j)
            totals[slot] += more
            accs[slot] += part
        for slot, piece in enumerate((lo, hi)):
            o_st[pl.ds(offset(piece), piece_len), :] = (accs[slot] / jnp.sum(totals[slot], axis=1, keepdims=True)).astype(jnp.bfloat16)
        for i in range(2 * per_half):
            tt = i
            rows = pl.ds(pl.multiple_of(p * 2 * piece_len + i * tokens, tokens), tokens)
            dcl, dtl = (p - c + cp) % cp, (tt - t + tp) % tp
            pl.when(dcl + dtl > 0)(o_copy(rows, dcl, dtl, p, tt).start)

            @pl.when(dcl + dtl == 0)
            def _():
                lanes = pl.ds(pl.multiple_of(unit_head * head_dim, 128), head_dim)
                o_rows[unit_seq, :, lanes] = o_st[rows]

    for dc in (1, cp - 1, 2):
        lane_y[dc].wait_recv()
        lane_mate[dc].start()
    bulk_wave(2)
    bulk_wave(3)
    for i in range(8):
        bulk_sent['p%d' % i].wait_recv()
    for copy in lane_mate.values():
        copy.wait_recv()
    first_rows = pl.ds(0, tokens)
    o_all = [o_copy(first_rows, dc, dt, (c + dc) % cp, (t + dt) % tp) for dc, dt in peers]
    for copy in o_all:
        copy.wait_recv()

    full = tp * heads * head_dim

    @pl.loop(0, hidden // 256)
    def _(n):
        at = pl.ds(pl.multiple_of(n * 256, 256), 256)
        a = jnp.dot(o_rows[...].reshape(2 * tokens, full), wo[:, :, :, at].reshape(full, 256), preferred_element_type=jnp.float32)
        h_ref[:, :, at] = (xg[t, :, :, at].astype(jnp.float32) + a.reshape(2, tokens, 256)).astype(jnp.bfloat16)

    for copy in list(x_sent.values()) + list(bulk_sent.values()) + list(strip_sent.values()) + list(lane_y.values()) + list(lane_mate.values()) + o_all:
        copy.wait_send()
    for dc in (1, cp - 1, 2):
        for tt in range(tp):
            u_copy(dc, tt).wait_send()


def run_front(act_in, w_query, w_key, w_value, w_out, cp, tp, heads):
    n_micro, tokens, hidden = act_in.shape
    head_dim = w_out.shape[1]
    half_rows = tokens * tp
    rows = cp * half_rows
    bf16 = jnp.bfloat16
    any_spec = pl.BlockSpec(memory_space=pl.ANY)
    dma = pltpu.SemaphoreType.DMA
    vmem = [(tp, n_micro, tokens, hidden), (tp // 2, 2, heads * head_dim, hidden), (hidden, heads * 3 * head_dim), (rows, 3 * head_dim), (tp, n_micro, tokens, heads * 3 * head_dim)]
    piece = half_rows // 2
    return pl.pallas_call(
        functools.partial(front_body, cp, tp, heads),
        out_shape=jax.ShapeDtypeStruct(act_in.shape, bf16),
        in_specs=[any_spec] * 5,
        out_specs=pl.BlockSpec(memory_space=pltpu.VMEM),
        scratch_shapes=[pltpu.VMEM(s, bf16) for s in vmem]
        + [pltpu.VMEM((2 * cp + 1, piece, piece), jnp.float32), pltpu.VMEM((rows, head_dim), bf16), pltpu.VMEM((n_micro, tokens, tp * heads * head_dim), bf16)]
        + [pltpu.VMEM((2, piece, 128), jnp.float32), pltpu.VMEM((2, piece, 128), jnp.float32), pltpu.VMEM((2, piece, head_dim), jnp.float32), pltpu.VMEM((3, hidden, heads, head_dim), bf16)]
        + [dma((6,)), dma((2, 14)), dma((2, 14)), dma((2, 14)), dma((2, cp)), dma((2, cp)), dma((2, cp, tp)), dma((2, cp, tp))],
        compiler_params=pltpu.CompilerParams(collective_id=2, has_side_effects=True, vmem_limit_bytes=56 << 20),
        cost_estimate=pl.CostEstimate(flops=8 * rows * hidden * head_dim * 3, bytes_accessed=20 << 20, transcendentals=0),
    )(act_in, w_query, w_key, w_value, w_out.reshape(heads * head_dim, hidden))


def expert_body(cp, tp, cap, h_ref, ids_ref, pick_ref, g_ref, wg_hbm, wu_hbm, wd_hbm, y_ref,
                ids_x, ids_y, g0, g1, s0, s1, e0, e1, z0, z1, b0, b1, f0, f1, wg, wu, wd, rows_in, act, mixed, w_sem,
                idx_sem, idy_sem, ring_x, ring_y, hop_y, hop_x, ret_y, ret_x, fin_x, fin_y):
    d, c, t = lax.axis_index('data'), lax.axis_index('cp'), lax.axis_index('tp')
    tokens, hidden = h_ref.shape[1], h_ref.shape[2]
    ff = wg.shape[1]
    nx = tp // 2
    x, k = t // 2, t % 2
    order = sorted(range(cp), key=lambda i: min(i, cp - i))
    seg = tp * cap
    half = tokens // 2

    weights = [pltpu.make_async_copy(a, b, w_sem.at[i]) for i, (a, b) in enumerate(((wg_hbm, wg), (wu_hbm, wu), (wd_hbm, wd)))]
    for copy in weights:
        copy.start()

    def device(dc, dx, dk):
        return (d, (c + dc) % cp, ((x + dx) % nx) * 2 + (k + dk) % 2)

    row_peers = [(dx, dk) for dx in order for dk in (0, 1) if dx or dk]
    col_peers = [(dc, dk) for dc in order for dk in (0, 1) if dc or dk]
    barrier = pltpu.get_barrier_semaphore()
    peers = [(0, dx, dk) for dx, dk in row_peers] + [(dc, 0, dk) for dc, dk in col_peers if dc]
    for peer in peers:
        pl.semaphore_signal(barrier, inc=1, device_id=device(*peer), device_id_type=MESH_ID)
    pl.semaphore_wait(barrier, len(peers))

    def send(src, dst, sems, key, target):
        return pltpu.make_async_remote_copy(src_ref=src, dst_ref=dst, send_sem=sems.at[(0,) + key], recv_sem=sems.at[(1,) + key], device_id=target, device_id_type=MESH_ID)

    started = []

    def go(*args):
        copy = send(*args)
        copy.start()
        started.append(copy)
        return copy

    ids_sent = {}
    for i in order[1:]:
        ids_sent[0, i] = go(ids_ref, ids_x.at[x], idx_sem, (i,), device(0, i, 0))
        ids_sent[1, i] = go(ids_ref, ids_y.at[c], idy_sem, (i,), device(i, 0, 0))

    parts = (pl.ds(0, half), pl.ds(half, half))
    ahead = (device(0, 1, 0), device(1, 0, 0))
    behind = (device(0, nx - 1, 0), device(cp - 1, 0, 0))
    here, size = (x, c), (nx, cp)
    held, sems = (g0, g1), (ring_x, ring_y)
    ring = {}
    for b in range(2):
        ring[b, 'r0'] = go(h_ref.at[b, parts[0]], held[b].at[here[b], parts[0]], sems[b], (0,), ahead[b])
        ring[b, 'l0'] = go(h_ref.at[b, parts[1]], held[b].at[here[b], parts[1]], sems[b], (1,), behind[b])
        ring[b, 'r1'] = go(h_ref.at[b, parts[1]], held[b].at[here[b], parts[1]], sems[b], (2,), ahead[b])
        ring[b, 'l1'] = go(h_ref.at[b, parts[0]], held[b].at[here[b], parts[0]], sems[b], (3,), behind[b])

    def relay(b):
        prev, nxt = (here[b] + size[b] - 1) % size[b], (here[b] + 1) % size[b]
        ring[b, 'r0'].wait_recv()
        ring[b, 'r2'] = go(held[b].at[prev, parts[0]], held[b].at[prev, parts[0]], sems[b], (4,), ahead[b])
        ring[b, 'l0'].wait_recv()
        ring[b, 'l2'] = go(held[b].at[nxt, parts[1]], held[b].at[nxt, parts[1]], sems[b], (5,), behind[b])

    slot_row = lax.broadcasted_iota(jnp.int32, (seg, tokens), 0)
    group = 2 * cap
    wanted = ((slot_row // group * (tp * cap) + x * group + slot_row % group).astype(jnp.float32), (slot_row + c * seg).astype(jnp.float32))
    hop = {}

    def stage(b, step):
        back = order[step]
        src = (here[b] + size[b] - back) % size[b]
        out = (s0, s1)[b]
        if step:
            ids_sent[b, back].wait_recv()
            ids = (ids_x, ids_y)[b][src]
        else:
            ids = ids_ref[...]
        hit = (ids[2 * b:2 * b + 1] == wanted[b]) | (ids[2 * b + 1:2 * b + 2] == wanted[b])
        sel = jnp.where(hit, 1.0, 0.0).astype(jnp.bfloat16)

        @pl.loop(0, hidden // 512)
        def _(n):
            at = pl.ds(pl.multiple_of(n * 512, 512), 512)
            rows = held[b][src, :, at] if step else h_ref[b, :, at]
            got = jnp.dot(sel, rows, preferred_element_type=jnp.float32).astype(jnp.bfloat16)
            out[step, :, :, :, at] = got.reshape(out.shape[1:4] + (512,))

        if b == 0:
            for dc, dk in col_peers:
                target = device(dc, 0, dk)
                hop[0, step, dc, dk] = go(s0.at[step, target[1], (k + dk) % 2], e0.at[src, c, k], hop_y, (step, dc, dk), target)
            e0[src, c, k] = s0[step, c, k]
        else:
            for dx, dk in row_peers:
                target = device(0, dx, dk)
                hop[1, step, dx, dk] = go(s1.at[step, (x + dx) % nx, (k + dk) % 2], e1.at[src, x, k], hop_x, (step, dx, dk), target)
            e1[src, x, k] = s1[step, x, k]

    stage(0, 0)
    stage(1, 0)
    relay(0)
    relay(1)
    for b in range(2):
        ring[b, 'r1'].wait_recv()
        stage(b, 1)
    for b in range(2):
        ring[b, 'l1'].wait_recv()
        stage(b, 2)
    for b in range(2):
        ring[b, 'r2'].wait_recv()
        ring[b, 'l2'].wait_recv()
        stage(b, 3)
    for copy in weights:
        copy.wait()

    def hidden_tile(at, width):
        both = jnp.dot(rows_in[...], jnp.concatenate([wg[:, at], wu[:, at]], axis=1), preferred_element_type=jnp.float32)
        gate, up = both[:, :width], both[:, width:]
        act[:, at] = (jax.nn.silu(gate) * up).astype(jnp.bfloat16)

    def run_expert():
        @pl.loop(0, ff // 256)
        def _(n):
            hidden_tile(pl.ds(pl.multiple_of(n * 256, 256), 256), 256)

        if ff % 256:
            hidden_tile(pl.ds(ff // 256 * 256, ff % 256), ff % 256)

        @pl.loop(0, hidden // 512)
        def _(n):
            at = pl.ds(pl.multiple_of(n * 512, 512), 512)
            rows_in[:, at] = jnp.dot(act[...], wd[:, at], preferred_element_type=jnp.float32).astype(jnp.bfloat16)

    ret = {}
    for step in range(cp):
        xs, cs = (x + nx - order[step]) % nx, (c + cp - order[step]) % cp
        for dc, dk in col_peers:
            hop[0, step, dc, dk].wait_recv()
        for dx, dk in row_peers:
            hop[1, step, dx, dk].wait_recv()
        rows_in[0:seg] = e0[xs].reshape(seg, hidden)
        rows_in[seg:2 * seg] = e1[cs].reshape(seg, hidden)
        run_expert()
        z0[step] = rows_in[0:seg].reshape(cp, 2, cap, hidden)
        z1[step] = rows_in[seg:2 * seg].reshape(nx, 2, cap, hidden)
        for dc, dk in col_peers:
            target = device(dc, 0, dk)
            ret[0, step, dc, dk] = go(z0.at[step, target[1], (k + dk) % 2], b0.at[step, c, k], ret_y, (step, dc, dk), target)
        b0[step, c, k] = z0[step, c, k]
        for dx, dk in row_peers:
            target = device(0, dx, dk)
            ret[1, step, dx, dk] = go(z1.at[step, (x + dx) % nx, (k + dk) % 2], b1.at[step, x, k], ret_x, (step, dx, dk), target)
        b1[step, x, k] = z1[step, x, k]

    fin = {}
    for step in range(cp):
        back = order[step]
        for dc, dk in col_peers:
            ret[0, step, dc, dk].wait_recv()
        if step:
            fin[0, step] = go(b0.at[step], f0.at[x], fin_x, (step,), device(0, nx - back, 0))
        for dx, dk in row_peers:
            ret[1, step, dx, dk].wait_recv()
        if step:
            fin[1, step] = go(b1.at[step], f1.at[c], fin_y, (step,), device(cp - back, 0, 0))

    for step in range(cp):
        if step:
            fin[0, step].wait_recv()
            fin[1, step].wait_recv()

        @pl.loop(0, hidden // 512)
        def _(n):
            at = pl.ds(pl.multiple_of(n * 512, 512), 512)
            for b in range(2):
                src = (here[b] + order[step]) % size[b]
                rows = (f0, f1)[b][src, :, :, :, at] if step else (b0, b1)[b][0, :, :, :, at]
                pick = pick_ref[b, :, pl.ds(pl.multiple_of(src * seg, seg), seg)]
                got = jnp.dot(pick, rows.reshape(seg, 512), preferred_element_type=jnp.float32)
                if step:
                    got += mixed[b, :, at]
                if step < cp - 1:
                    mixed[b, :, at] = got
                else:
                    both = g_ref[b, :, 0:1] * got[:tokens] + g_ref[b, :, 1:2] * got[tokens:]
                    y_ref[b, :, at] = (h_ref[b, :, at].astype(jnp.float32) + both).astype(jnp.bfloat16)

    for copy in started:
        copy.wait_send()


def run_experts(mid_rows, ids, pick, route_gates, w_gate, w_up, w_down, cp, tp, cap):
    n_micro, tokens, hidden = mid_rows.shape
    ff = w_gate.shape[1]
    bf16 = jnp.bfloat16
    nx = tp // 2
    by_x, by_y = (cp, cp, 2, cap, hidden), (cp, nx, 2, cap, hidden)
    rows = 2 * (tp * cap)
    vmem = pl.BlockSpec(memory_space=pltpu.VMEM)
    any_spec = pl.BlockSpec(memory_space=pl.ANY)
    dma = pltpu.SemaphoreType.DMA
    return pl.pallas_call(
        functools.partial(expert_body, cp, tp, cap),
        out_shape=jax.ShapeDtypeStruct(mid_rows.shape, bf16),
        in_specs=[vmem] * 4 + [any_spec] * 3,
        out_specs=vmem,
        scratch_shapes=[pltpu.VMEM((nx,) + ids.shape, jnp.float32), pltpu.VMEM((cp,) + ids.shape, jnp.float32)]
        + [pltpu.VMEM((nx, tokens, hidden), bf16), pltpu.VMEM((cp, tokens, hidden), bf16)]
        + [pltpu.VMEM(s, bf16) for s in (by_x, by_y) * 5]
        + [pltpu.VMEM((hidden, ff), bf16), pltpu.VMEM((hidden, ff), bf16), pltpu.VMEM((ff, hidden), bf16)]
        + [pltpu.VMEM((rows, hidden), bf16), pltpu.VMEM((rows, ff), bf16), pltpu.VMEM((n_micro, 2 * tokens, hidden), jnp.float32)]
        + [dma((3,)), dma((2, nx)), dma((2, cp)), dma((2, 6)), dma((2, 6)), dma((2, cp, cp, 2)), dma((2, cp, nx, 2)), dma((2, cp, cp, 2)), dma((2, cp, nx, 2)), dma((2, cp)), dma((2, cp))],
        compiler_params=pltpu.CompilerParams(collective_id=1, has_side_effects=True, vmem_limit_bytes=60 << 20),
        cost_estimate=pl.CostEstimate(flops=6 * 4 * rows * hidden * ff, bytes_accessed=6 * hidden * ff, transcendentals=0),
    )(mid_rows, ids, pick, route_gates, w_gate, w_up, w_down)


def solution(mesh):
    cp_size = mesh.shape['cp']
    tp_size = mesh.shape['tp']
    experts = cp_size * tp_size
    row_spec = P(None, ('data', 'cp', 'tp'), None)
    head_spec = P(None, 'tp', None)
    out_spec = P('tp', None, None)
    expert_spec = P(('cp', 'tp'), None, None)

    def device_step(act_in, route_ids, route_gates, w_query, w_key, w_value, w_out, w_gate, w_up, w_down):
        n_micro, tokens, hidden = act_in.shape
        heads, head_dim = w_query.shape[1], w_query.shape[2]
        mid_rows = run_front(act_in, w_query, w_key, w_value, w_out, cp_size, tp_size, heads)

        capacity = (4 * tokens) // experts
        slots = experts * capacity
        flat_ids = route_ids.reshape(n_micro, 2 * tokens)
        hits = (flat_ids[..., None] == jnp.arange(experts)).astype(jnp.bfloat16)
        before = (jnp.arange(2 * tokens)[:, None] > jnp.arange(2 * tokens)[None, :]).astype(jnp.bfloat16)
        rank = jnp.einsum('ij,bje->bie', before, hits, preferred_element_type=jnp.float32)
        slot_rank = jnp.sum(rank * hits.astype(jnp.float32), axis=-1).astype(jnp.int32)
        col, row = flat_ids % tp_size, flat_ids // tp_size
        chip_slot = ((col // 2 * cp_size + row) * 2 + col % 2) * capacity
        base_slot = jnp.where(jnp.arange(n_micro)[:, None] == 0, chip_slot, flat_ids * capacity)
        by_choice = lambda v: v.reshape(n_micro, tokens, 2).transpose(0, 2, 1).reshape(n_micro, 2 * tokens)
        pick = (by_choice(base_slot + slot_rank)[:, :, None] == jnp.arange(slots)).astype(jnp.bfloat16)
        ids = by_choice(flat_ids * capacity + slot_rank).astype(jnp.float32).reshape(2 * n_micro, tokens)
        ids = jnp.concatenate([ids, ids], axis=0)
        return run_experts(mid_rows, ids, pick, route_gates, w_gate[0], w_up[0], w_down[0], cp_size, tp_size, capacity)

    return jax.shard_map(device_step, mesh=mesh, in_specs=(row_spec, row_spec, row_spec, head_spec, head_spec, head_spec, out_spec, expert_spec, expert_spec, expert_spec), out_specs=row_spec, check_vma=False)
```

time: 230 us -> 200 us (0.87)
  Pallas kernels: 216 us -> 192 us
  other arithmetic: 7.8 us -> 2.32 us
    pallas_call x1, Pallas kernels: 120 us -> 104 us  [run_experts(): pl.pallas_call(functools.partial(expert_body, cp, tp, cap), out_shape=jax...]
    pallas_call x1, Pallas kernels: 95.7 us -> 88.9 us  [run_front(): pl.pallas_call(functools.partial(front_body, cp, tp, heads), out_shape=ja...]
    concatenate x1, other arithmetic: 5.82 us -> 0.6 us  [device_step(): ids = jnp.concatenate([ids, ids], axis=0)]
    unnamed x9 -> x4, local copies, waits for them, and re-layouts: 5.54 us -> 4.59 us
where the time goes in v4:
time: 200 us
  Pallas kernels  192 us (96%)
  local copies, waits for them, and re-layouts  4.94 us (2%)
  other arithmetic  2.32 us (1%)
    pallas_call x1, Pallas kernels, run_experts(): pl.pallas_call(functools.partial(expert_body, cp, tp, cap), out_shape=jax...  104 us
    pallas_call x1, Pallas kernels, run_front(): pl.pallas_call(functools.partial(front_body, cp, tp, heads), out_shape=ja...  88.9 us
    unnamed x4, local copies, waits for them, and re-layouts  4.59 us

profile of v4, /device:TPU:97, one launch (start us, length us, event | category | flops | bytes accessed | tf_op | source)
XLA Modules:
  0.0 200.0 jit_solution(4035541307145734370)
XLA Ops:
  0.0 1.5 copy.46.g_ref
  1.5 0.8 copy.43
  2.3 0.1 eq.41
  2.4 0.2 fusion.1
  2.7 0.1 convert_element_type.31
  2.8 0.1 copy.44
  2.9 0.8 add_bitcast_fusion
  3.7 0.6 pad_maximum_fusion.ids_ref
  4.3 0.9 fusion.2.pick_ref
  5.2 88.9 %shard_map.100.h_ref = bf16[2,128,2048]{2,1,0:T(8,128)(2,1)} custom-call(bf16[2,128,2048]{2,1,0:T(8,128)(2,1)} %x_hbm.1, bf16[2048,2,128]{2,1,0:T(2,128)(2,1)} %wq_hbm.1, bf16[2048,2,128]{2,1,0:T(2,128)(2,1)} %wk_hbm.1, bf16[2048,2,128]{2,1,0:T(2,128)(2,1)} %wv_hbm.1, bf16[256,2048]{1,0:T(8,128)(2,1)} %bitcast.27), custom_call_target="tpu_custom_call" | custom-call | flops 25769803776 | bytes 20971520 | tf_op jit(solution)/shard_map/pallas_call | solution.py:307
  94.1 103.6 %shard_map.101 = bf16[2,128,2048]{2,1,0:T(8,128)(2,1)} custom-call(bf16[2,128,2048]{2,1,0:T(8,128)(2,1)} %shard_map.100.h_ref, f32[8,128]{1,0:T(8,128)} %pad_maximum_fusion.ids_ref, bf16[2,256,512]{2,1,0:T(8,128)(2,1)} %fusion.2.pick_ref, f32[2,128,2]{2,1,0:T(8,128)} %copy.46.g_ref, bf16[2048,1408]{1,0:T(8,128)(2,1)} %bitcast.24, ...), custom_call_target="tpu_custom_call" | custom-call | flops 17716740096 | bytes 17301504 | tf_op jit(solution)/shard_map/pallas_call | solution.py:521
  197.7 2.3 %copy.51 = bf16[2,128,2048]{2,1,0:T(8,128)(2,1)} copy(bf16[2,128,2048]{2,1,0:T(8,128)(2,1)} %shard_map.101) | data formatting | bytes 2097152
  (3 shorter events, 0.0 us)

commit v5 on v4

--- a/solution.py
+++ b/solution.py
@@ -13,8 +13,8 @@
 MESH_ID = pl.DeviceIdType.MESH
 
 
-def front_body(cp, tp, heads, x_hbm, wq_hbm, wk_hbm, wv_hbm, wo_hbm, h_ref, xg, wo, w, u, q_out, s_ref, o_st, o_rows,
-               peaks, totals, accs, raw, in_sem, x_sem, bulk_sem, strip_sem, lane_sem, mate_sem, u_sem, o_sem):
+def front_body(cp, tp, heads, strip_len, x_hbm, wq_hbm, wk_hbm, wv_hbm, wo_hbm, h_ref, xg, wo, w, u, q_out, s_ref, o_st, o_rows,
+               peaks, totals, accs, raw, a_sum, in_sem, x_sem, bulk_sem, strip_sem, lane_sem, mate_sem, u_sem, o_sem):
     d, c, t = lax.axis_index('data'), lax.axis_index('cp'), lax.axis_index('tp')
     nx = tp // 2
     x, k = t // 2, t % 2
@@ -28,8 +28,8 @@
     mine, other = k, 1 - k
     mate = 2 * x + other
 
-    split = wo_hbm.shape[0] - 16 * cp
-    strip_rows = pl.ds(split + 16 * c, 16)
+    split = wo_hbm.shape[0] - strip_len * cp
+    strip_rows = pl.ds(split + strip_len * c, strip_len)
     loads = [pltpu.make_async_copy(x_hbm, xg.at[t], in_sem.at[0]), pltpu.make_async_copy(wq_hbm, raw.at[0], in_sem.at[1]), pltpu.make_async_copy(wo_hbm.at[pl.ds(0, split)], wo.at[x, k, pl.ds(0, split)], in_sem.at[2]),
              pltpu.make_async_copy(wo_hbm.at[strip_rows], wo.at[x, k, strip_rows], in_sem.at[3]),
              pltpu.make_async_copy(wk_hbm, raw.at[1], in_sem.at[4]), pltpu.make_async_copy(wv_hbm, raw.at[2], in_sem.at[5])]
@@ -87,10 +87,10 @@
         return wo.at[src // 2, src % 2, pl.ds(part * part_rows, part_rows)]
 
     def strip(src, part):
-        return wo.at[src // 2, src % 2, pl.ds(split + 16 * c, 16), pl.ds(part * (hidden // 2), hidden // 2)]
+        return wo.at[src // 2, src % 2, pl.ds(split + strip_len * c, strip_len), pl.ds(part * (hidden // 2), hidden // 2)]
 
     def lane(q):
-        return wo.at[:, k, pl.ds(split + 16 * q, 16)]
+        return wo.at[:, k, pl.ds(split + strip_len * q, strip_len)]
 
     x_sent, x_wave = ring(lambda src, part: xg.at[src, part], x_sem, True)
     bulk_sent, bulk_wave = ring(bulk, bulk_sem, True)
@@ -116,21 +116,24 @@
             lanes = pl.ds(pl.multiple_of(c % heads * width, 128), width)
             u[rows] = q_out[tt, s, :, lanes]
 
-    loads[0].wait()
-    x_wave(0)
-    loads[3].wait()
-    strip_wave(0)
-    for i in (1, 4, 5):
-        loads[i].wait()
-
-    @pl.loop(0, hidden // 32)
-    def _(i):
-        at = pl.ds(pl.multiple_of(i * 32, 32), 32)
-        for j in range(3):
+    def relayout(j, load):
+        load.wait()
+
+        @pl.loop(0, hidden // 32)
+        def _(i):
+            at = pl.ds(pl.multiple_of(i * 32, 32), 32)
             flat = raw[j, at].reshape(32, heads * head_dim)
             for n in range(heads):
                 w[at, n * width + j * head_dim:n * width + (j + 1) * head_dim] = flat[:, n * head_dim:(n + 1) * head_dim]
 
+    loads[3].wait()
+    strip_wave(0)
+    relayout(0, loads[1])
+    strip_wave(1)
+    loads[0].wait()
+    x_wave(0)
+    relayout(1, loads[4])
+    relayout(2, loads[5])
     project(t, 0)
     project(t, 1)
     for s, name in ((0, 'p0'), (1, 'p1')):
@@ -144,7 +147,6 @@
     x_sent['p3'].wait_recv()
     project(right + other, 1)
     x_wave(2)
-    strip_wave(1)
     loads[2].wait()
     bulk_wave(0)
     project(left + mine, 1)
@@ -269,23 +271,39 @@
         lane_y[dc].wait_recv()
         lane_mate[dc].start()
     bulk_wave(2)
-    bulk_wave(3)
-    for i in range(8):
-        bulk_sent['p%d' % i].wait_recv()
+    first_rows = pl.ds(0, tokens)
+    o_all = [o_copy(first_rows, dc, dt, (c + dc) % cp, (t + dt) % tp) for dc, dt in peers]
+    per_chip = 2 * heads * head_dim
+
+    def contract(dx, names):
+        xs = (x + nx - dx) % nx
+        for name in names:
+            bulk_sent[name].wait_recv()
+        for dc in range(cp):
+            for dk in range(2):
+                if dx or dc or dk:
+                    dt = (t + tp - 2 * xs - (k + dk) % 2) % tp
+                    o_copy(first_rows, dc, dt, (c + dc) % cp, (t + dt) % tp).wait_recv()
+
+        @pl.loop(0, hidden // 512)
+        def _(n):
+            at = pl.ds(pl.multiple_of(n * 512, 512), 512)
+            o_part = o_rows[:, :, pl.ds(pl.multiple_of(xs * per_chip, per_chip), per_chip)].reshape(2 * tokens, per_chip)
+            a = jnp.dot(o_part, wo[xs, :, :, at].reshape(per_chip, 512), preferred_element_type=jnp.float32)
+            if dx:
+                a += a_sum[:, at]
+            if dx == 2:
+                h_ref[:, :, at] = (xg[t, :, :, at].astype(jnp.float32) + a.reshape(2, tokens, 512)).astype(jnp.bfloat16)
+            else:
+                a_sum[:, at] = a
+
     for copy in lane_mate.values():
         copy.wait_recv()
-    first_rows = pl.ds(0, tokens)
-    o_all = [o_copy(first_rows, dc, dt, (c + dc) % cp, (t + dt) % tp) for dc, dt in peers]
-    for copy in o_all:
-        copy.wait_recv()
-
-    full = tp * heads * head_dim
-
-    @pl.loop(0, hidden // 256)
-    def _(n):
-        at = pl.ds(pl.multiple_of(n * 256, 256), 256)
-        a = jnp.dot(o_rows[...].reshape(2 * tokens, full), wo[:, :, :, at].reshape(full, 256), preferred_element_type=jnp.float32)
-        h_ref[:, :, at] = (xg[t, :, :, at].astype(jnp.float32) + a.reshape(2, tokens, 256)).astype(jnp.bfloat16)
+    contract(0, ('p0', 'p1'))
+    bulk_wave(3)
+    contract(1, ('p2', 'p4'))
+    contract(nx - 1, ('p3', 'p5'))
+    contract(2, ('p6', 'p7'))
 
     for copy in list(x_sent.values()) + list(bulk_sent.values()) + list(strip_sent.values()) + list(lane_y.values()) + list(lane_mate.values()) + o_all:
         copy.wait_send()
@@ -305,21 +323,21 @@
     vmem = [(tp, n_micro, tokens, hidden), (tp // 2, 2, heads * head_dim, hidden), (hidden, heads * 3 * head_dim), (rows, 3 * head_dim), (tp, n_micro, tokens, heads * 3 * head_dim)]
     piece = half_rows // 2
     return pl.pallas_call(
-        functools.partial(front_body, cp, tp, heads),
+        functools.partial(front_body, cp, tp, heads, 16),
         out_shape=jax.ShapeDtypeStruct(act_in.shape, bf16),
         in_specs=[any_spec] * 5,
         out_specs=pl.BlockSpec(memory_space=pltpu.VMEM),
         scratch_shapes=[pltpu.VMEM(s, bf16) for s in vmem]
         + [pltpu.VMEM((2 * cp + 1, piece, piece), jnp.float32), pltpu.VMEM((rows, head_dim), bf16), pltpu.VMEM((n_micro, tokens, tp * heads * head_dim), bf16)]
-        + [pltpu.VMEM((2, piece, 128), jnp.float32), pltpu.VMEM((2, piece, 128), jnp.float32), pltpu.VMEM((2, piece, head_dim), jnp.float32), pltpu.VMEM((3, hidden, heads, head_dim), bf16)]
+        + [pltpu.VMEM((2, piece, 128), jnp.float32), pltpu.VMEM((2, piece, 128), jnp.float32), pltpu.VMEM((2, piece, head_dim), jnp.float32), pltpu.VMEM((3, hidden, heads, head_dim), bf16), pltpu.VMEM((n_micro * tokens, hidden), jnp.float32)]
         + [dma((6,)), dma((2, 14)), dma((2, 14)), dma((2, 14)), dma((2, cp)), dma((2, cp)), dma((2, cp, tp)), dma((2, cp, tp))],
         compiler_params=pltpu.CompilerParams(collective_id=2, has_side_effects=True, vmem_limit_bytes=56 << 20),
         cost_estimate=pl.CostEstimate(flops=8 * rows * hidden * head_dim * 3, bytes_accessed=20 << 20, transcendentals=0),
     )(act_in, w_query, w_key, w_value, w_out.reshape(heads * head_dim, hidden))
 
 
-def expert_body(cp, tp, cap, h_ref, ids_ref, pick_ref, g_ref, wg_hbm, wu_hbm, wd_hbm, y_ref,
-                ids_x, ids_y, g0, g1, s0, s1, e0, e1, z0, z1, b0, b1, f0, f1, wg, wu, wd, rows_in, act, mixed, w_sem,
+def expert_body(cp, tp, cap, h_ref, route_ref, g_ref, wg_hbm, wu_hbm, wd_hbm, y_ref,
+                ids_ref, pos_ref, ids_x, ids_y, g0, g1, s0, s1, e0, e1, z0, z1, b0, b1, f0, f1, wg, wu, wd, rows_in, act, mixed, w_sem,
                 idx_sem, idy_sem, ring_x, ring_y, hop_y, hop_x, ret_y, ret_x, fin_x, fin_y):
     d, c, t = lax.axis_index('data'), lax.axis_index('cp'), lax.axis_index('tp')
     tokens, hidden = h_ref.shape[1], h_ref.shape[2]
@@ -343,6 +361,22 @@
     peers = [(0, dx, dk) for dx, dk in row_peers] + [(dc, 0, dk) for dc, dk in col_peers if dc]
     for peer in peers:
         pl.semaphore_signal(barrier, inc=1, device_id=device(*peer), device_id_type=MESH_ID)
+    experts = cp * tp
+    expert = lax.broadcasted_iota(jnp.int32, (experts, tokens), 0)
+    before = lax.broadcasted_iota(jnp.int32, (tokens, tokens), 0) < lax.broadcasted_iota(jnp.int32, (tokens, tokens), 1)
+    before = jnp.where(before, 1.0, 0.0).astype(jnp.bfloat16)
+    e_col, e_row = expert % tp, expert // tp
+    bases = ((((e_col // 2 * cp + e_row) * 2 + e_col % 2) * cap).astype(jnp.float32), (expert * cap).astype(jnp.float32))
+    ids_ref[...] = jnp.zeros_like(ids_ref)
+    for b in range(2):
+        used = jnp.zeros((experts, 1), jnp.float32)
+        for i in range(2):
+            row = 2 * b + i
+            hit = jnp.where(expert == route_ref[b, i:i + 1, :], 1.0, 0.0)
+            rank = jnp.dot(hit.astype(jnp.bfloat16), before, preferred_element_type=jnp.float32) + used
+            used = used + jnp.sum(hit, axis=1, keepdims=True)
+            ids_ref[row:row + 1] = jnp.sum(hit * (rank + bases[1]), axis=0, keepdims=True)
+            pos_ref[row:row + 1] = jnp.sum(hit * (rank + bases[b]), axis=0, keepdims=True)
     pl.semaphore_wait(barrier, len(peers))
 
     def send(src, dst, sems, key, target):
@@ -483,7 +517,14 @@
         if step:
             fin[1, step] = go(b1.at[step], f1.at[c], fin_y, (step,), device(cp - back, 0, 0))
 
+    slot_f = slot_row.astype(jnp.float32)
+    gates = [[jnp.transpose(jnp.broadcast_to(g_ref[b, i:i + 1, :], (tokens, tokens))) for i in range(2)] for b in range(2)]
     for step in range(cp):
+        srcs = [(here[b] + order[step]) % size[b] for b in range(2)]
+        picks = []
+        for b in range(2):
+            want = slot_f + (srcs[b] * seg).astype(jnp.float32)
+            picks.append(jnp.concatenate([jnp.transpose(jnp.where(pos_ref[2 * b + i:2 * b + i + 1] == want, 1.0, 0.0)) for i in range(2)], axis=0).astype(jnp.bfloat16))
         if step:
             fin[0, step].wait_recv()
             fin[1, step].wait_recv()
@@ -492,23 +533,22 @@
         def _(n):
             at = pl.ds(pl.multiple_of(n * 512, 512), 512)
             for b in range(2):
-                src = (here[b] + order[step]) % size[b]
-                rows = (f0, f1)[b][src, :, :, :, at] if step else (b0, b1)[b][0, :, :, :, at]
-                pick = pick_ref[b, :, pl.ds(pl.multiple_of(src * seg, seg), seg)]
-                got = jnp.dot(pick, rows.reshape(seg, 512), preferred_element_type=jnp.float32)
+                rows = (f0, f1)[b][srcs[b], :, :, :, at] if step else (b0, b1)[b][0, :, :, :, at]
+                got = jnp.dot(picks[b], rows.reshape(seg, 512), preferred_element_type=jnp.float32)
                 if step:
                     got += mixed[b, :, at]
                 if step < cp - 1:
                     mixed[b, :, at] = got
                 else:
-                    both = g_ref[b, :, 0:1] * got[:tokens] + g_ref[b, :, 1:2] * got[tokens:]
+                    g0_tile, g1_tile = (jnp.concatenate([g] * (512 // tokens), axis=1) for g in gates[b])
+                    both = g0_tile * got[:tokens] + g1_tile * got[tokens:]
                     y_ref[b, :, at] = (h_ref[b, :, at].astype(jnp.float32) + both).astype(jnp.bfloat16)
 
     for copy in started:
         copy.wait_send()
 
 
-def run_experts(mid_rows, ids, pick, route_gates, w_gate, w_up, w_down, cp, tp, cap):
+def run_experts(mid_rows, route, gates, w_gate, w_up, w_down, cp, tp, cap):
     n_micro, tokens, hidden = mid_rows.shape
     ff = w_gate.shape[1]
     bf16 = jnp.bfloat16
@@ -521,9 +561,9 @@
     return pl.pallas_call(
         functools.partial(expert_body, cp, tp, cap),
         out_shape=jax.ShapeDtypeStruct(mid_rows.shape, bf16),
-        in_specs=[vmem] * 4 + [any_spec] * 3,
+        in_specs=[vmem] * 3 + [any_spec] * 3,
         out_specs=vmem,
-        scratch_shapes=[pltpu.VMEM((nx,) + ids.shape, jnp.float32), pltpu.VMEM((cp,) + ids.shape, jnp.float32)]
+        scratch_shapes=[pltpu.VMEM(s, jnp.float32) for s in ((8, tokens), (8, tokens), (nx, 8, tokens), (cp, 8, tokens))]
         + [pltpu.VMEM((nx, tokens, hidden), bf16), pltpu.VMEM((cp, tokens, hidden), bf16)]
         + [pltpu.VMEM(s, bf16) for s in (by_x, by_y) * 5]
         + [pltpu.VMEM((hidden, ff), bf16), pltpu.VMEM((hidden, ff), bf16), pltpu.VMEM((ff, hidden), bf16)]
@@ -531,7 +571,7 @@
         + [dma((3,)), dma((2, nx)), dma((2, cp)), dma((2, 6)), dma((2, 6)), dma((2, cp, cp, 2)), dma((2, cp, nx, 2)), dma((2, cp, cp, 2)), dma((2, cp, nx, 2)), dma((2, cp)), dma((2, cp))],
         compiler_params=pltpu.CompilerParams(collective_id=1, has_side_effects=True, vmem_limit_bytes=60 << 20),
         cost_estimate=pl.CostEstimate(flops=6 * 4 * rows * hidden * ff, bytes_accessed=6 * hidden * ff, transcendentals=0),
-    )(mid_rows, ids, pick, route_gates, w_gate, w_up, w_down)
+    )(mid_rows, route, gates, w_gate, w_up, w_down)
 
 
 def solution(mesh):
@@ -549,19 +589,8 @@
         mid_rows = run_front(act_in, w_query, w_key, w_value, w_out, cp_size, tp_size, heads)
 
         capacity = (4 * tokens) // experts
-        slots = experts * capacity
-        flat_ids = route_ids.reshape(n_micro, 2 * tokens)
-        hits = (flat_ids[..., None] == jnp.arange(experts)).astype(jnp.bfloat16)
-        before = (jnp.arange(2 * tokens)[:, None] > jnp.arange(2 * tokens)[None, :]).astype(jnp.bfloat16)
-        rank = jnp.einsum('ij,bje->bie', before, hits, preferred_element_type=jnp.float32)
-        slot_rank = jnp.sum(rank * hits.astype(jnp.float32), axis=-1).astype(jnp.int32)
-        col, row = flat_ids % tp_size, flat_ids // tp_size
-        chip_slot = ((col // 2 * cp_size + row) * 2 + col % 2) * capacity
-        base_slot = jnp.where(jnp.arange(n_micro)[:, None] == 0, chip_slot, flat_ids * capacity)
-        by_choice = lambda v: v.reshape(n_micro, tokens, 2).transpose(0, 2, 1).reshape(n_micro, 2 * tokens)
-        pick = (by_choice(base_slot + slot_rank)[:, :, None] == jnp.arange(slots)).astype(jnp.bfloat16)
-        ids = by_choice(flat_ids * capacity + slot_rank).astype(jnp.float32).reshape(2 * n_micro, tokens)
-        ids = jnp.concatenate([ids, ids], axis=0)
-        return run_experts(mid_rows, ids, pick, route_gates, w_gate[0], w_up[0], w_down[0], cp_size, tp_size, capacity)
+        route = jnp.transpose(route_ids, (0, 2, 1))
+        gates = jnp.transpose(route_gates, (0, 2, 1))
+        return run_experts(mid_rows, route, gates, w_gate[0], w_up[0], w_down[0], cp_size, tp_size, capacity)
 
     return jax.shard_map(device_step, mesh=mesh, in_specs=(row_spec, row_spec, row_spec, head_spec, head_spec, head_spec, out_spec, expert_spec, expert_spec, expert_spec), out_specs=row_spec, check_vma=False)

time: 200 us -> 194 us (0.970)
  local copies, waits for them, and re-layouts: 4.94 us -> 2.3 us
  other arithmetic: 2.32 us -> 0 us
    unnamed x4 -> x1, local copies, waits for them, and re-layouts: 4.59 us -> 2.3 us
    pallas_call x1, Pallas kernels: 104 us -> 101 us  [run_experts(): pl.pallas_call(functools.partial(expert_body, cp, tp, cap), out_shape=jax...]
where the time goes in v5:
time: 194 us; the launch traced here: 193 us
  Pallas kernels  191 us (98%)
  local copies, waits for them, and re-layouts  2.3 us (1%)
    pallas_call x1, Pallas kernels, run_experts(): pl.pallas_call(functools.partial(expert_body, cp, tp, cap), out_shape=jax...  101 us
    pallas_call x1, Pallas kernels, run_front(): pl.pallas_call(functools.partial(front_body, cp, tp, heads, 16), out_shap...  89.8 us

profile of v5, /device:TPU:97, one launch (start us, length us, event | category | flops | bytes accessed | tf_op | source)
XLA Modules:
  0.0 193.5 jit_solution(14184549641653655849)
XLA Ops:
  0.0 89.8 %shard_map.100.h_ref = bf16[2,128,2048]{2,1,0:T(8,128)(2,1)} custom-call(bf16[2,128,2048]{2,1,0:T(8,128)(2,1)} %x_hbm.1, bf16[2048,2,128]{2,1,0:T(2,128)(2,1)} %wq_hbm.1, bf16[2048,2,128]{2,1,0:T(2,128)(2,1)} %wk_hbm.1, bf16[2048,2,128]{2,1,0:T(2,128)(2,1)} %wv_hbm.1, bf16[256,2048]{1,0:T(8,128)(2,1)} %bitcast.9), custom_call_target="tpu_custom_call" | custom-call | flops 25769803776 | bytes 20971520 | tf_op jit(solution)/shard_map/pallas_call | solution.py:325
  89.8 101.4 %shard_map.101 = bf16[2,128,2048]{2,1,0:T(8,128)(2,1)} custom-call(bf16[2,128,2048]{2,1,0:T(8,128)(2,1)} %shard_map.100.h_ref, s32[2,2,128]{2,1,0:T(2,128)} %bitcast.10, f32[2,2,128]{2,1,0:T(2,128)} %bitcast.11, bf16[2048,1408]{1,0:T(8,128)(2,1)} %bitcast.6, bf16[2048,1408]{1,0:T(8,128)(2,1)} %bitcast.7, bf16[1408,2048]{1,0:T(8,128)(2,1)} %bitcast.8), custom_call_target="tpu_custom_call" | custom-call | flops 17716740096 | bytes 17301504 | tf_op jit(solution)/shard_map/pallas_call | solution.py:561
  191.2 2.3 %copy.12 = bf16[2,128,2048]{2,1,0:T(8,128)(2,1)} copy(bf16[2,128,2048]{2,1,0:T(8,128)(2,1)} %shard_map.101) | data formatting | bytes 2097152

commit v6 on v5

--- a/solution.py
+++ b/solution.py
@@ -119,21 +119,19 @@
     def relayout(j, load):
         load.wait()
 
-        @pl.loop(0, hidden // 32)
+        @pl.loop(0, hidden // 128)
         def _(i):
-            at = pl.ds(pl.multiple_of(i * 32, 32), 32)
-            flat = raw[j, at].reshape(32, heads * head_dim)
+            at = pl.ds(pl.multiple_of(i * 128, 128), 128)
+            flat = raw[j, at].reshape(128, heads * head_dim)
             for n in range(heads):
                 w[at, n * width + j * head_dim:n * width + (j + 1) * head_dim] = flat[:, n * head_dim:(n + 1) * head_dim]
 
+    loads[0].wait()
+    x_wave(0)
     loads[3].wait()
     strip_wave(0)
-    relayout(0, loads[1])
-    strip_wave(1)
-    loads[0].wait()
-    x_wave(0)
-    relayout(1, loads[4])
-    relayout(2, loads[5])
+    for j, i in enumerate((1, 4, 5)):
+        relayout(j, loads[i])
     project(t, 0)
     project(t, 1)
     for s, name in ((0, 'p0'), (1, 'p1')):
@@ -147,6 +145,7 @@
     x_sent['p3'].wait_recv()
     project(right + other, 1)
     x_wave(2)
+    strip_wave(1)
     loads[2].wait()
     bulk_wave(0)
     project(left + mine, 1)
@@ -203,7 +202,8 @@
     gap = col - row
 
     @pl.loop(0, cp)
-    def _(p):
+    def _(turn):
+        p = (c + 1 + turn) % cp
         lo, hi = p, pieces - 1 - p
 
         def place(j):
@@ -257,8 +257,8 @@
         for slot, piece in enumerate((lo, hi)):
             o_st[pl.ds(offset(piece), piece_len), :] = (accs[slot] / jnp.sum(totals[slot], axis=1, keepdims=True)).astype(jnp.bfloat16)
         for i in range(2 * per_half):
-            tt = i
-            rows = pl.ds(pl.multiple_of(p * 2 * piece_len + i * tokens, tokens), tokens)
+            tt = (t + 1 + i) % tp
+            rows = pl.ds(pl.multiple_of(p * 2 * piece_len + tt * tokens, tokens), tokens)
             dcl, dtl = (p - c + cp) % cp, (tt - t + tp) % tp
             pl.when(dcl + dtl > 0)(o_copy(rows, dcl, dtl, p, tt).start)
 

time: 194 us -> 189 us (0.974)
  Pallas kernels: 191 us -> 186 us
    pallas_call x1, Pallas kernels: 101 us -> 95.1 us  [run_experts(): pl.pallas_call(functools.partial(expert_body, cp, tp, cap), out_shape=jax...]
where the time goes in v6:
time: 189 us
  Pallas kernels  186 us (98%)
  local copies, waits for them, and re-layouts  2.3 us (1%)
    pallas_call x1, Pallas kernels, run_experts(): pl.pallas_call(functools.partial(expert_body, cp, tp, cap), out_shape=jax...  95.1 us
    pallas_call x1, Pallas kernels, run_front(): pl.pallas_call(functools.partial(front_body, cp, tp, heads, 16), out_shap...  91.3 us

profile of v6, /device:TPU:97, one launch (start us, length us, event | category | flops | bytes accessed | tf_op | source)
XLA Modules:
  0.0 188.7 jit_solution(6759436684373345788)
XLA Ops:
  0.0 91.3 %shard_map.100.h_ref = bf16[2,128,2048]{2,1,0:T(8,128)(2,1)} custom-call(bf16[2,128,2048]{2,1,0:T(8,128)(2,1)} %x_hbm.1, bf16[2048,2,128]{2,1,0:T(2,128)(2,1)} %wq_hbm.1, bf16[2048,2,128]{2,1,0:T(2,128)(2,1)} %wk_hbm.1, bf16[2048,2,128]{2,1,0:T(2,128)(2,1)} %wv_hbm.1, bf16[256,2048]{1,0:T(8,128)(2,1)} %bitcast.9), custom_call_target="tpu_custom_call" | custom-call | flops 25769803776 | bytes 20971520 | tf_op jit(solution)/shard_map/pallas_call | solution.py:325
  91.3 95.1 %shard_map.101 = bf16[2,128,2048]{2,1,0:T(8,128)(2,1)} custom-call(bf16[2,128,2048]{2,1,0:T(8,128)(2,1)} %shard_map.100.h_ref, s32[2,2,128]{2,1,0:T(2,128)} %bitcast.10, f32[2,2,128]{2,1,0:T(2,128)} %bitcast.11, bf16[2048,1408]{1,0:T(8,128)(2,1)} %bitcast.6, bf16[2048,1408]{1,0:T(8,128)(2,1)} %bitcast.7, bf16[1408,2048]{1,0:T(8,128)(2,1)} %bitcast.8), custom_call_target="tpu_custom_call" | custom-call | flops 17716740096 | bytes 17301504 | tf_op jit(solution)/shard_map/pallas_call | solution.py:561
  186.4 2.3 %copy.12 = bf16[2,128,2048]{2,1,0:T(8,128)(2,1)} copy(bf16[2,128,2048]{2,1,0:T(8,128)(2,1)} %shard_map.101) | data formatting | bytes 2097152

commit v7 on v6

--- a/solution.py
+++ b/solution.py
@@ -132,35 +132,34 @@
     strip_wave(0)
     for j, i in enumerate((1, 4, 5)):
         relayout(j, loads[i])
-    project(t, 0)
-    project(t, 1)
-    for s, name in ((0, 'p0'), (1, 'p1')):
-        x_sent[name].wait_recv()
-        project(mate, s)
+    odd = c % 2
+
+    def either(one, two):
+        project(jnp.where(odd == 0, one[0], two[0]), jnp.where(odd == 0, one[1], two[1]))
+        project(jnp.where(odd == 0, two[0], one[0]), jnp.where(odd == 0, two[1], one[1]))
+
+    either((t, 0), (t, 1))
+    x_sent['p0'].wait_recv()
+    x_sent['p1'].wait_recv()
+    either((mate, 0), (mate, 1))
     x_wave(1)
-    project(left + mine, 0)
-    project(right + mine, 1)
+    either((left + mine, 0), (right + mine, 1))
     x_sent['p2'].wait_recv()
-    project(left + other, 0)
     x_sent['p3'].wait_recv()
-    project(right + other, 1)
+    either((left + other, 0), (right + other, 1))
     x_wave(2)
     strip_wave(1)
     loads[2].wait()
     bulk_wave(0)
-    project(left + mine, 1)
-    project(right + mine, 0)
+    either((left + mine, 1), (right + mine, 0))
     x_sent['p4'].wait_recv()
-    project(left + other, 1)
     x_sent['p5'].wait_recv()
-    project(right + other, 0)
+    either((left + other, 1), (right + other, 0))
     x_wave(3)
-    project(far + mine, 0)
-    project(far + mine, 1)
+    either((far + mine, 0), (far + mine, 1))
     x_sent['p6'].wait_recv()
-    project(far + other, 0)
     x_sent['p7'].wait_recv()
-    project(far + other, 1)
+    either((far + other, 0), (far + other, 1))
     strip_wave(2)
     strip_wave(3)
     for dc in (1, cp - 1, 2):
@@ -574,6 +573,15 @@
     )(mid_rows, route, gates, w_gate, w_up, w_down)
 
 
+def hand_out_body(src, dst):
+    dst[...] = src[...]
+
+
+def hand_out(rows):
+    vmem = pl.BlockSpec((1,) + rows.shape[1:], lambda i: (i, 0, 0))
+    return pl.pallas_call(hand_out_body, grid=rows.shape[:1], out_shape=jax.ShapeDtypeStruct(rows.shape, rows.dtype), in_specs=[vmem], out_specs=vmem)(rows)
+
+
 def solution(mesh):
     cp_size = mesh.shape['cp']
     tp_size = mesh.shape['tp']
@@ -591,6 +599,7 @@
         capacity = (4 * tokens) // experts
         route = jnp.transpose(route_ids, (0, 2, 1))
         gates = jnp.transpose(route_gates, (0, 2, 1))
-        return run_experts(mid_rows, route, gates, w_gate[0], w_up[0], w_down[0], cp_size, tp_size, capacity)
+        rows_out = run_experts(mid_rows, route, gates, w_gate[0], w_up[0], w_down[0], cp_size, tp_size, capacity)
+        return hand_out(rows_out)
 
     return jax.shard_map(device_step, mesh=mesh, in_specs=(row_spec, row_spec, row_spec, head_spec, head_spec, head_spec, out_spec, expert_spec, expert_spec, expert_spec), out_specs=row_spec, check_vma=False)

time: 189 us -> 188 us (level)
  local copies, waits for them, and re-layouts: 2.3 us -> 0 us
  Pallas kernels: 186 us -> 188 us
    unnamed x1 -> x0, local copies, waits for them, and re-layouts: 2.3 us -> none
    pallas_call x0 -> x1, Pallas kernels: none -> 2.05 us  [hand_out(): pl.pallas_call(hand_out_body, grid=rows.shape[:1], out_shape=jax.ShapeDty...]
where the time goes in v7:
time: 188 us
  Pallas kernels  188 us (100%)
    pallas_call x1, Pallas kernels, run_experts(): pl.pallas_call(functools.partial(expert_body, cp, tp, cap), out_shape=jax...  94.7 us
    pallas_call x1, Pallas kernels, run_front(): pl.pallas_call(functools.partial(front_body, cp, tp, heads, 16), out_shap...  90.9 us

profile of v7, /device:TPU:97, one launch (start us, length us, event | category | flops | bytes accessed | tf_op | source)
XLA Modules:
  0.0 187.8 jit_solution(10115841481165979891)
XLA Ops:
  0.0 90.9 %shard_map.100.h_ref = bf16[2,128,2048]{2,1,0:T(8,128)(2,1)} custom-call(bf16[2,128,2048]{2,1,0:T(8,128)(2,1)} %x_hbm.1, bf16[2048,2,128]{2,1,0:T(2,128)(2,1)} %wq_hbm.1, bf16[2048,2,128]{2,1,0:T(2,128)(2,1)} %wk_hbm.1, bf16[2048,2,128]{2,1,0:T(2,128)(2,1)} %wv_hbm.1, bf16[256,2048]{1,0:T(8,128)(2,1)} %bitcast.9), custom_call_target="tpu_custom_call" | custom-call | flops 25769803776 | bytes 20971520 | tf_op jit(solution)/shard_map/pallas_call | solution.py:324
  90.9 94.7 %shard_map.101.src = bf16[2,128,2048]{2,1,0:T(8,128)(2,1)} custom-call(bf16[2,128,2048]{2,1,0:T(8,128)(2,1)} %shard_map.100.h_ref, s32[2,2,128]{2,1,0:T(2,128)} %bitcast.10, f32[2,2,128]{2,1,0:T(2,128)} %bitcast.11, bf16[2048,1408]{1,0:T(8,128)(2,1)} %bitcast.6, bf16[2048,1408]{1,0:T(8,128)(2,1)} %bitcast.7, bf16[1408,2048]{1,0:T(8,128)(2,1)} %bitcast.8), custom_call_target="tpu_custom_call" | custom-call | flops 17716740096 | bytes 17301504 | tf_op jit(solution)/shard_map/pallas_call | solution.py:560
  185.7 2.1 %shard_map.102 = bf16[2,128,2048]{2,1,0:T(8,128)(2,1)} custom-call(bf16[2,128,2048]{2,1,0:T(8,128)(2,1)} %shard_map.101.src), custom_call_target="tpu_custom_call" | custom-call | tf_op jit(solution)/shard_map/pallas_call | solution.py:582
